TPU v7x, 32 devices: a whole 2x2x4 slice. The times are simulated.
32 devices in a mesh: alpha: 8 (over y, x, core), beta: 4 (over z).
Axes of the slice: x: 2, y: 2, z: 4, core: 2. Of those that a mesh axis runs over, the one named last changes fastest.
Arguments:
- ci_vector: bfloat16 [1024, 2048], P('alpha', 'beta'), may hold values from -6 to 6
- alpha_tiles: bfloat16 [8, 8, 4, 128, 128], P(None, 'alpha'), may hold values from -0.25 to 0.25
- alpha_list: int32 [8, 8, 4], P(None, 'alpha'), may hold values from 0 to 7, as said below
- alpha_count: int32 [8, 8], P(None, 'alpha'), may hold values from 1 to 4, as said below
- beta_tiles: bfloat16 [8, 16, 4, 128, 128], P(None, 'beta'), may hold values from -0.09375 to 0.09375
- beta_target: int32 [8, 16, 4], P(None, 'beta'), may hold values from 0 to 15
- alpha_diag: float32 [1024], P('alpha'), may hold values from -6 to 6
- beta_diag: float32 [2048], P('beta'), may hold values from -6 to 6
Outputs:
- sigma_vector: float32 [1024, 2048], P('alpha', 'beta')
Inputs may be any that keep to these rules, and one draw needn't show every extreme that they name: `alpha_list`: the 4 entries of one factor and block are distinct alpha blocks within 3 blocks of that block. `alpha_count`: some alpha block has 4 live slots in every factor.
All inputs are finite; a program needn't handle non-finite values.
Results may differ from a plain program's by a relative error of at most 0.007.
Values may be sent and summed in bfloat16 or wider, within the bound.
No kernel may reach another device: no remote copies, remote signals or barrier semaphores. Data moves between devices by JAX's collectives and lax.ppermute only.
A program may use at most 64 MiB of HBM per device.

v0:
```python
import jax
import jax.numpy as jnp
from jax import lax
from jax.experimental import pallas as pl
from jax.experimental.pallas import tpu as pltpu
from jax.sharding import PartitionSpec as P


BAND = 3
WARM_FLOPS = 2 * 10**10


def band_window(ci_vector):
    length = lax.axis_size("alpha")
    held = {BAND: ci_vector}
    for offset in range(-BAND, BAND + 1):
        if offset:
            pairs = [(i, i - offset) for i in range(length) if 0 <= i - offset < length]
            held[offset + BAND] = lax.ppermute(ci_vector, "alpha", pairs)
    return held, lambda block, own: block - own + BAND, ()


def cube_window(ci_vector):
    length = lax.axis_size("alpha")

    def near(i, source):
        return abs(i - source) <= BAND

    held, relayed = {0: ci_vector}, []
    for k in range(2, length, 2):
        even = [i for i in range(length) if near(i, i ^ k)]
        odd = [i for i in range(length) if near(i, i ^ k ^ 1)]
        if even:
            taking = {i for i in range(length) if near(i, i ^ k) or near(i ^ 1, i ^ k)}
            pairs = [(i ^ (k if i in taking else 1), i) for i in range(length)]
            held[k] = lax.ppermute(ci_vector, "alpha", pairs)
            if odd:
                relayed.append(k)
        elif odd:
            pairs = [(i ^ (k ^ 1 if i in odd else 0), i) for i in range(length)]
            held[k + 1] = lax.ppermute(ci_vector, "alpha", pairs)
    swap = [(i, i ^ 1) for i in range(length)]
    held[1] = lax.ppermute(ci_vector, "alpha", swap)
    for k in relayed:
        held[k + 1] = lax.ppermute(held[k], "alpha", swap)
    return held, lambda block, own: block ^ own, ()


def warm_kernel(counts_from, counts_to):
    counts_to[...] = counts_from[...]


def couple_kernel(
    sizes, place_of, sources, counts, targets, held, alpha_tiles, beta_tiles, outs, window, total
):
    factors, alpha_slots, local_blocks, beta_slots, groups, by_xor = sizes
    tile_size = total.shape[1]
    own_block, own_group = lax.axis_index("alpha"), lax.axis_index("beta")
    for place, piece in held.items():
        window[place] = piece[...]
    for block in range(total.shape[0]):
        total[block] = jnp.zeros(total.shape[1:], jnp.float32)
    for factor in range(factors):
        places = [place_of(sources[0, slot, factor], own_block) for slot in range(alpha_slots)]
        stacked = jnp.concatenate([window[place] for place in places], axis=0)
        tiles = [alpha_tiles[factor, 0, slot] for slot in range(alpha_slots)]
        live = [jnp.where(slot < counts[0, factor], tile, jnp.zeros_like(tile)) for slot, tile in enumerate(tiles)]
        coupled = jnp.dot(
            jnp.concatenate(live, axis=1), stacked, preferred_element_type=jnp.float32
        ).astype(jnp.bfloat16)
        for block in range(local_blocks):
            source = coupled[:, block * tile_size : (block + 1) * tile_size]
            tiles = [beta_tiles[factor, block, slot] for slot in range(beta_slots)]
            added = jnp.dot(source, jnp.concatenate(tiles, axis=1), preferred_element_type=jnp.float32)
            for slot in range(beta_slots):
                target = targets[block, slot, factor]
                group = target // local_blocks
                away = (group ^ own_group) if by_xor else lax.rem(group - own_group + groups, groups)
                place = away * local_blocks + lax.rem(target, local_blocks)
                total[place] += added[:, slot * tile_size : (slot + 1) * tile_size]
    for away in range(groups):
        for block in range(local_blocks):
            value = total[away * local_blocks + block].astype(jnp.bfloat16)
            outs[away][:, block * tile_size : (block + 1) * tile_size] = value


def shards(
    ci_vector, alpha_tiles, alpha_list, alpha_count, beta_tiles, beta_target, alpha_diag, beta_diag
):
    tile_size, columns = ci_vector.shape
    factors, _, alpha_slots = alpha_list.shape
    _, local_blocks, beta_slots = beta_target.shape
    length, groups = lax.axis_size("alpha"), lax.axis_size("beta")
    held, place_of, _ = window_of(length)(ci_vector)
    by_xor = groups & (groups - 1) == 0
    sizes = (factors, alpha_slots, local_blocks, beta_slots, groups, by_xor)
    vmem = pl.BlockSpec(memory_space=pltpu.VMEM)
    smem = pl.BlockSpec(memory_space=pltpu.SMEM)
    tile_bytes = (alpha_tiles.size + beta_tiles.size) * 2

    counts = jnp.transpose(alpha_count, (1, 0))
    counts = pl.pallas_call(
        warm_kernel,
        out_shape=jax.ShapeDtypeStruct(counts.shape, counts.dtype),
        in_specs=[vmem],
        out_specs=vmem,
        compiler_params=pltpu.CompilerParams(vmem_limit_bytes=2**20),
        cost_estimate=pl.CostEstimate(flops=WARM_FLOPS, bytes_accessed=counts.size, transcendentals=0),
        name="warm",
    )(counts)

    def body(sources, counts, targets, *refs):
        n = len(held)
        pieces = dict(zip(held, refs[:n]))
        a_ref, b_ref, *outs = refs[n:-2]
        couple_kernel(sizes, place_of, sources, counts, targets, pieces, a_ref, b_ref, outs, *refs[-2:])

    own, *far = pl.pallas_call(
        body,
        out_shape=[jax.ShapeDtypeStruct((tile_size, columns), jnp.bfloat16)] * groups,
        in_specs=[smem] * 3 + [vmem] * (len(held) + 2),
        out_specs=[vmem] * groups,
        scratch_shapes=[
            pltpu.VMEM((max(held) + 1, tile_size, columns), jnp.bfloat16),
            pltpu.VMEM((groups * local_blocks, tile_size, tile_size), jnp.float32),
        ],
        compiler_params=pltpu.CompilerParams(vmem_limit_bytes=20 * 2**20),
        cost_estimate=pl.CostEstimate(
            flops=2 * factors * tile_size * columns * tile_size * (alpha_slots + beta_slots),
            bytes_accessed=tile_bytes,
            transcendentals=0,
        ),
        name="couple",
    )(
        jnp.transpose(alpha_list, (1, 2, 0)),
        counts,
        jnp.transpose(beta_target, (1, 2, 0)),
        *held.values(),
        alpha_tiles,
        beta_tiles,
    )
    summed = own.astype(jnp.float32)
    for away in far_order(groups):
        if by_xor:
            pairs = [(i, i ^ away) for i in range(groups)]
        else:
            pairs = [(i, (i + away) % groups) for i in range(groups)]
        received = lax.ppermute(far[away - 1], "beta", pairs)
        summed = summed + received.astype(jnp.float32)
    return summed + (alpha_diag[:, None] + beta_diag[None, :]) * ci_vector.astype(jnp.float32)


def far_order(groups):
    return [*range(2, groups), *range(1, min(groups, 2))]


def window_of(length):
    return cube_window if length & (length - 1) == 0 and length <= 2 * (BAND + 1) else band_window


def solution(mesh):
    placed = (
        P("alpha", "beta"),
        P(None, "alpha", None, None, None),
        P(None, "alpha", None),
        P(None, "alpha"),
        P(None, "beta", None, None, None),
        P(None, "beta", None),
        P("alpha"),
        P("beta"),
    )

    return jax.shard_map(shards, mesh=mesh, in_specs=placed, out_specs=P("alpha", "beta"), check_vma=False)
```

profile of v0, /device:TPU:0, one launch (start us, length us, event | category | flops | bytes accessed | tf_op | source)
XLA Modules:
  0.0 32.2 jit_solution(2082037059315672839)
XLA Ops:
  0.0 0.5 %collective-permute-start.2 = (bf16[128,512]{1,0:T(8,128)(2,1)}, bf16[128,512]{1,0:T(8,128)(2,1)S(1)}, u32[]{:S(2)}, u32[]{:S(2)}) collective-permute-start(bf16[128,512]{1,0:T(8,128)(2,1)} %refs_0_.1), channel_id=1, source_target_pairs={{4,0},{0,4},{16,8},{20,12},{8,16},{12,20},{28,24},{24,28},{5,1},{1... | collective-permute-start | bytes 393224 | tf_op jit(solution)/shard_map/ppermute | solution.py:36
  0.5 4.0 %collective-permute-start = (bf16[128,512]{1,0:T(8,128)(2,1)}, bf16[128,512]{1,0:T(8,128)(2,1)S(1)}, u32[]{:S(2)}, u32[]{:S(2)}) collective-permute-start(bf16[128,512]{1,0:T(8,128)(2,1)} %refs_0_.1), channel_id=1, source_target_pairs={{8,0},{12,4},{0,8},{4,12},{24,16},{28,20},{16,24},{20,28},{9,1},{1... | collective-permute-start | bytes 393224 | tf_op jit(solution)/shard_map/ppermute | solution.py:36
  4.5 0.0 collective-permute-start.3
  4.5 1.6 %collective-permute-start.1 = (bf16[128,512]{1,0:T(8,128)(2,1)}, bf16[128,512]{1,0:T(8,128)(2,1)S(1)}, u32[]{:S(2)}, u32[]{:S(2)}) collective-permute-start(bf16[128,512]{1,0:T(8,128)(2,1)} %refs_0_.1), channel_id=1, source_target_pairs={{0,0},{16,4},{8,8},{24,12},{4,16},{20,20},{12,24},{28,28},{1,1},{1... | collective-permute-start | bytes 393224 | tf_op jit(solution)/shard_map/ppermute | solution.py:41
  6.0 0.0 collective-permute-done.2.refs_3_
  6.0 0.9 %collective-permute-start.5 = (bf16[128,512]{1,0:T(8,128)(2,1)S(1)}, bf16[128,512]{1,0:T(8,128)(2,1)S(1)}, u32[]{:S(2)}, u32[]{:S(2)}) collective-permute-start(bf16[128,512]{1,0:T(8,128)(2,1)S(1)} %collective-permute-done.2.refs_3_), channel_id=1, source_target_pairs={{0,4},{4,0},{8,12},{12,8},{16,20},{20,16},{24,28},{28,24},{1,5},{5... | collective-permute-start | bytes 393224 | tf_op jit(solution)/shard_map/ppermute | solution.py:45
  7.0 3.7 %collective-permute-done.refs_1_ = bf16[128,512]{1,0:T(8,128)(2,1)S(1)} collective-permute-done((bf16[128,512]{1,0:T(8,128)(2,1)}, bf16[128,512]{1,0:T(8,128)(2,1)S(1)}, u32[]{:S(2)}, u32[]{:S(2)}) %collective-permute-start) | collective-permute-done | bytes 131104 | tf_op jit(solution)/shard_map/ppermute | solution.py:36
  10.7 0.0 collective-permute-start.4
  10.7 0.0 copy-start.5
  10.7 0.7 %copy-done.5 = s32[8,1]{0,1:T(1,128)S(1)} copy-done((s32[8,1]{0,1:T(1,128)S(1)}, s32[8,1]{0,1:T(1,128)}, u32[]{:S(2)}) %copy-start.5) | copy-done | bytes 56
  11.3 0.0 copy-start
  11.4 0.0 copy-start.1
  11.4 0.0 copy-start.2
  11.4 0.0 copy-start.3
  11.4 0.0 copy-start.4
  11.4 0.0 copy-start.6
  11.4 0.0 copy-start.7
  11.4 0.0 collective-permute-done.3.refs_4_
  11.4 0.0 collective-permute-done.1.refs_2_
  11.4 0.0 collective-permute-done.5.refs_6_
  11.4 0.6 %collective-permute-done.4.refs_5_ = bf16[128,512]{1,0:T(8,128)(2,1)S(1)} collective-permute-done((bf16[128,512]{1,0:T(8,128)(2,1)S(1)}, bf16[128,512]{1,0:T(8,128)(2,1)S(1)}, u32[]{:S(2)}, u32[]{:S(2)}) %collective-permute-start.4) | collective-permute-done | bytes 131104 | tf_op jit(solution)/shard_map/ppermute | solution.py:45
  12.0 1.5 %copy-done = bf16[8,4,4,128,128]{4,3,2,1,0:T(8,128)(2,1)S(1)} copy-done((bf16[8,4,4,128,128]{4,3,2,1,0:T(8,128)(2,1)S(1)}, bf16[8,4,4,128,128]{4,3,2,1,0:T(8,128)(2,1)}, u32[]{:S(2)}) %copy-start) | copy-done | bytes 4194328
  13.5 0.3 copy-done.1
  13.8 0.0 copy-done.2
  13.8 0.0 copy-done.3
  13.8 0.0 copy-done.4
  13.8 3.6 %couple.1 = (bf16[128,512]{1,0:T(8,128)(2,1)S(1)}, bf16[128,512]{1,0:T(8,128)(2,1)S(1)}, bf16[128,512]{1,0:T(8,128)(2,1)S(1)}, bf16[128,512]{1,0:T(8,128)(2,1)S(1)}) custom-call(s32[1,4,8]{2,1,0:T(4,128)S(1)} %bitcast.4, s32[1,8]{1,0:T(1,128)S(1)} %warm.1.counts, s32[4,4,8]{2,1,0:T(4,128)S(1)} %bitcast.3, bf16[128,512]{1,0:T(8,128)(2,1)S(1)} %copy-done.2, ...), custom_call_target="tpu_custom_call" | custom-call | flops 1073741824 | bytes 5242880 | tf_op jit(solution)/shard_map/couple/pallas_call | solution.py:118
  17.5 2.6 %collective-permute-start.6 = (bf16[128,512]{1,0:T(8,128)(2,1)S(1)}, bf16[128,512]{1,0:T(8,128)(2,1)S(1)}, u32[]{:S(2)}, u32[]{:S(2)}) collective-permute-start(bf16[128,512]{1,0:T(8,128)(2,1)S(1)} %get-tuple-element.10), channel_id=1, source_target_pairs={{0,2},{1,3},{2,0},{3,1},{4,6},{5,7},{6,4},{7,5},{8,10},{9,11},{10,... | collective-permute-start | bytes 393224 | tf_op jit(solution)/shard_map/ppermute | solution.py:148
  20.1 1.3 %collective-permute-start.7 = (bf16[128,512]{1,0:T(8,128)(2,1)S(1)}, bf16[128,512]{1,0:T(8,128)(2,1)S(1)}, u32[]{:S(2)}, u32[]{:S(2)}) collective-permute-start(bf16[128,512]{1,0:T(8,128)(2,1)S(1)} %get-tuple-element.11), channel_id=1, source_target_pairs={{0,3},{1,2},{2,1},{3,0},{4,7},{5,6},{6,5},{7,4},{8,11},{9,10},{10,... | collective-permute-start | bytes 393224 | tf_op jit(solution)/shard_map/ppermute | solution.py:148
  21.5 0.2 collective-permute-start.8
  21.7 8.8 %collective-permute-done.6 = bf16[128,512]{1,0:T(8,128)(2,1)S(1)} collective-permute-done((bf16[128,512]{1,0:T(8,128)(2,1)S(1)}, bf16[128,512]{1,0:T(8,128)(2,1)S(1)}, u32[]{:S(2)}, u32[]{:S(2)}) %collective-permute-start.6) | collective-permute-done | bytes 131104 | tf_op jit(solution)/shard_map/ppermute | solution.py:148
  30.5 0.0 collective-permute-done.7
  30.5 0.9 %collective-permute-done.8 = bf16[128,512]{1,0:T(8,128)(2,1)S(1)} collective-permute-done((bf16[128,512]{1,0:T(8,128)(2,1)S(1)}, bf16[128,512]{1,0:T(8,128)(2,1)S(1)}, u32[]{:S(2)}, u32[]{:S(2)}) %collective-permute-start.8) | collective-permute-done | bytes 131104 | tf_op jit(solution)/shard_map/ppermute | solution.py:148
  31.3 0.0 copy-done.6
  31.3 0.0 copy-done.7
  31.4 0.8 %multiply_add_fusion = f32[128,512]{1,0:T(8,128)} fusion(bf16[128,512]{1,0:T(8,128)(2,1)S(1)} %copy-done.2, bf16[128,512]{1,0:T(8,128)(2,1)S(1)} %collective-permute-done.8, bf16[128,512]{1,0:T(8,128)(2,1)S(1)} %collective-permute-done.7, bf16[128,512]{1,0:T(8,128)(2,1)S(1)} %collective-permute-done.6, bf16[128,512]{1,0:T(8,128)(2,1)S(1)} %get-tuple-element.9, ...), kind=kLoop, calls=%fused_computation | loop fusion | flops 720896 | bytes 920064 | tf_op jit(solution)/shard_map/add | solution.py:150
  (1 shorter events, 0.0 us)
Async XLA Ops:
  0.0 6.0 %collective-permute-start.2 = (bf16[128,512]{1,0:T(8,128)(2,1)}, bf16[128,512]{1,0:T(8,128)(2,1)S(1)}, u32[]{:S(2)}, u32[]{:S(2)}) collective-permute-start(bf16[128,512]{1,0:T(8,128)(2,1)} %refs_0_.1), channel_id=1, source_target_pairs={{4,0},{0,4},{16,8},{20,12},{8,16},{12,20},{28,24},{24,28},{5,1},{1... | collective-permute-start | bytes 393224 | tf_op jit(solution)/shard_map/ppermute | solution.py:36
  0.5 10.2 %collective-permute-start = (bf16[128,512]{1,0:T(8,128)(2,1)}, bf16[128,512]{1,0:T(8,128)(2,1)S(1)}, u32[]{:S(2)}, u32[]{:S(2)}) collective-permute-start(bf16[128,512]{1,0:T(8,128)(2,1)} %refs_0_.1), channel_id=1, source_target_pairs={{8,0},{12,4},{0,8},{4,12},{24,16},{28,20},{16,24},{20,28},{9,1},{1... | collective-permute-start | bytes 393224 | tf_op jit(solution)/shard_map/ppermute | solution.py:36
  4.5 6.9 %collective-permute-start.3 = (bf16[128,512]{1,0:T(8,128)(2,1)}, bf16[128,512]{1,0:T(8,128)(2,1)S(1)}, u32[]{:S(2)}, u32[]{:S(2)}) collective-permute-start(bf16[128,512]{1,0:T(8,128)(2,1)} %refs_0_.1), channel_id=1, source_target_pairs={{0,4},{4,0},{8,12},{12,8},{16,20},{20,16},{24,28},{28,24},{1,5},{5... | collective-permute-start | bytes 393224 | tf_op jit(solution)/shard_map/ppermute | solution.py:43
  4.5 7.0 %collective-permute-start.1 = (bf16[128,512]{1,0:T(8,128)(2,1)}, bf16[128,512]{1,0:T(8,128)(2,1)S(1)}, u32[]{:S(2)}, u32[]{:S(2)}) collective-permute-start(bf16[128,512]{1,0:T(8,128)(2,1)} %refs_0_.1), channel_id=1, source_target_pairs={{0,0},{16,4},{8,8},{24,12},{4,16},{20,20},{12,24},{28,28},{1,1},{1... | collective-permute-start | bytes 393224 | tf_op jit(solution)/shard_map/ppermute | solution.py:41
  6.0 5.4 %collective-permute-start.5 = (bf16[128,512]{1,0:T(8,128)(2,1)S(1)}, bf16[128,512]{1,0:T(8,128)(2,1)S(1)}, u32[]{:S(2)}, u32[]{:S(2)}) collective-permute-start(bf16[128,512]{1,0:T(8,128)(2,1)S(1)} %collective-permute-done.2.refs_3_), channel_id=1, source_target_pairs={{0,4},{4,0},{8,12},{12,8},{16,20},{20,16},{24,28},{28,24},{1,5},{5... | collective-permute-start | bytes 393224 | tf_op jit(solution)/shard_map/ppermute | solution.py:45
  10.7 1.3 %collective-permute-start.4 = (bf16[128,512]{1,0:T(8,128)(2,1)S(1)}, bf16[128,512]{1,0:T(8,128)(2,1)S(1)}, u32[]{:S(2)}, u32[]{:S(2)}) collective-permute-start(bf16[128,512]{1,0:T(8,128)(2,1)S(1)} %collective-permute-done.refs_1_), channel_id=1, source_target_pairs={{0,4},{4,0},{8,12},{12,8},{16,20},{20,16},{24,28},{28,24},{1,5},{5... | collective-permute-start | bytes 393224 | tf_op jit(solution)/shard_map/ppermute | solution.py:45
  10.7 0.7 %copy-start.5 = (s32[8,1]{0,1:T(1,128)S(1)}, s32[8,1]{0,1:T(1,128)}, u32[]{:S(2)}) copy-start(s32[8,1]{0,1:T(1,128)} %param.11) | copy-start | bytes 100
  11.3 2.2 %copy-start = (bf16[8,4,4,128,128]{4,3,2,1,0:T(8,128)(2,1)S(1)}, bf16[8,4,4,128,128]{4,3,2,1,0:T(8,128)(2,1)}, u32[]{:S(2)}) copy-start(bf16[8,4,4,128,128]{4,3,2,1,0:T(8,128)(2,1)} %refs_8_.1) | copy-start | bytes 12582916
  11.4 2.5 %copy-start.1 = (bf16[8,1,4,128,128]{4,3,2,1,0:T(8,128)(2,1)S(1)}, bf16[8,1,4,128,128]{4,3,2,1,0:T(8,128)(2,1)}, u32[]{:S(2)}) copy-start(bf16[8,1,4,128,128]{4,3,2,1,0:T(8,128)(2,1)} %refs_7_.1) | copy-start | bytes 3145732
  11.4 2.5 %copy-start.2 = (bf16[128,512]{1,0:T(8,128)(2,1)S(1)}, bf16[128,512]{1,0:T(8,128)(2,1)}, u32[]{:S(2)}) copy-start(bf16[128,512]{1,0:T(8,128)(2,1)} %refs_0_.1) | copy-start | bytes 393220
  11.4 2.5 %copy-start.3 = (s32[8,4,4]{0,2,1:T(4,128)S(1)}, s32[8,4,4]{0,2,1:T(4,128)}, u32[]{:S(2)}) copy-start(s32[8,4,4]{0,2,1:T(4,128)} %param.13) | copy-start | bytes 1540
  11.4 2.5 %copy-start.4 = (s32[8,1,4]{0,2,1:T(4,128)S(1)}, s32[8,1,4]{0,2,1:T(4,128)}, u32[]{:S(2)}) copy-start(s32[8,1,4]{0,2,1:T(4,128)} %param.10) | copy-start | bytes 388
  11.4 20.0 %copy-start.6 = (f32[512]{0:T(512)S(1)}, f32[512]{0:T(512)}, u32[]{:S(2)}) copy-start(f32[512]{0:T(512)} %param.15) | copy-start | bytes 6148
  11.4 20.0 %copy-start.7 = (f32[128]{0:T(128)S(1)}, f32[128]{0:T(128)}, u32[]{:S(2)}) copy-start(f32[128]{0:T(128)} %param.14) | copy-start | bytes 1540
  17.5 13.0 %collective-permute-start.6 = (bf16[128,512]{1,0:T(8,128)(2,1)S(1)}, bf16[128,512]{1,0:T(8,128)(2,1)S(1)}, u32[]{:S(2)}, u32[]{:S(2)}) collective-permute-start(bf16[128,512]{1,0:T(8,128)(2,1)S(1)} %get-tuple-element.10), channel_id=1, source_target_pairs={{0,2},{1,3},{2,0},{3,1},{4,6},{5,7},{6,4},{7,5},{8,10},{9,11},{10,... | collective-permute-start | bytes 393224 | tf_op jit(solution)/shard_map/ppermute | solution.py:148
  20.1 10.4 %collective-permute-start.7 = (bf16[128,512]{1,0:T(8,128)(2,1)S(1)}, bf16[128,512]{1,0:T(8,128)(2,1)S(1)}, u32[]{:S(2)}, u32[]{:S(2)}) collective-permute-start(bf16[128,512]{1,0:T(8,128)(2,1)S(1)} %get-tuple-element.11), channel_id=1, source_target_pairs={{0,3},{1,2},{2,1},{3,0},{4,7},{5,6},{6,5},{7,4},{8,11},{9,10},{10,... | collective-permute-start | bytes 393224 | tf_op jit(solution)/shard_map/ppermute | solution.py:148
  21.5 9.9 %collective-permute-start.8 = (bf16[128,512]{1,0:T(8,128)(2,1)S(1)}, bf16[128,512]{1,0:T(8,128)(2,1)S(1)}, u32[]{:S(2)}, u32[]{:S(2)}) collective-permute-start(bf16[128,512]{1,0:T(8,128)(2,1)S(1)} %get-tuple-element.12), channel_id=1, source_target_pairs={{0,1},{1,0},{2,3},{3,2},{4,5},{5,4},{6,7},{7,6},{8,9},{9,8},{10,11... | collective-permute-start | bytes 393224 | tf_op jit(solution)/shard_map/ppermute | solution.py:148
where the time goes:
time: 32.5 us; the launch traced here: 32.2 us
  waiting for transfers between devices  14 us (43%)
  starting transfers between devices  11.2 us (34%)
  Pallas kernels  3.61 us (11%)
  local copies, waits for them, and re-layouts  2.48 us (8%)
  other arithmetic  0.81 us (2%)
    ppermute x3, waiting for transfers between devices, shards(): received = lax.ppermute(far[away - 1], 'beta', pairs)  9.67 us
    ppermute x2, starting transfers between devices, cube_window(): held[k] = lax.ppermute(ci_vector, 'alpha', pairs)  4.46 us
    ppermute x3, starting transfers between devices, shards(): received = lax.ppermute(far[away - 1], 'beta', pairs)  4.21 us
    ppermute x2, waiting for transfers between devices, cube_window(): held[k] = lax.ppermute(ci_vector, 'alpha', pairs)  3.73 us
    pallas_call x1, Pallas kernels, shards(): pl.pallas_call(body, out_shape=[jax.ShapeDtypeStruct((tile_size, columns)...  3.61 us
    unnamed x16, local copies, waits for them, and re-layouts  2.48 us
    ppermute x1, starting transfers between devices, cube_window(): held[k + 1] = lax.ppermute(ci_vector, 'alpha', pairs)  1.55 us
    ppermute x2, starting transfers between devices, cube_window(): held[k + 1] = lax.ppermute(held[k], 'alpha', swap)  0.95 us
  transfers between devices with their start and end apart: 9, of which 4 were waited for; matrix products, arithmetic and copies ran while one was open for 0% of the time, Pallas kernels for 0%

commit v1 on v0

--- a/solution.py
+++ b/solution.py
@@ -46,30 +46,41 @@
     return held, lambda block, own: block ^ own, ()
 
 
-def warm_kernel(counts_from, counts_to):
-    counts_to[...] = counts_from[...]
+def warm_kernel(out):
+    out[...] = jnp.zeros_like(out)
 
 
 def couple_kernel(
-    sizes, place_of, sources, counts, targets, held, alpha_tiles, beta_tiles, outs, window, total
+    sizes, place_of, tables_from, held, alpha_tiles, beta_tiles, outs, window, coupled, total, tables, semaphores
 ):
-    factors, alpha_slots, local_blocks, beta_slots, groups, by_xor = sizes
+    factors, alpha_slots, local_blocks, beta_slots, groups, by_xor, parts = sizes
     tile_size = total.shape[1]
     own_block, own_group = lax.axis_index("alpha"), lax.axis_index("beta")
+    copies = [
+        pltpu.make_async_copy(source, table, semaphores.at[i])
+        for i, (source, table) in enumerate(zip(tables_from, tables))
+    ]
+    for copy in copies:
+        copy.start()
+    sources, counts, targets = tables
     for place, piece in held.items():
         window[place] = piece[...]
     for block in range(total.shape[0]):
         total[block] = jnp.zeros(total.shape[1:], jnp.float32)
-    for factor in range(factors):
+    for copy in copies:
+        copy.wait()
+
+    def alpha(factor):
         places = [place_of(sources[0, slot, factor], own_block) for slot in range(alpha_slots)]
         stacked = jnp.concatenate([window[place] for place in places], axis=0)
         tiles = [alpha_tiles[factor, 0, slot] for slot in range(alpha_slots)]
         live = [jnp.where(slot < counts[0, factor], tile, jnp.zeros_like(tile)) for slot, tile in enumerate(tiles)]
-        coupled = jnp.dot(
-            jnp.concatenate(live, axis=1), stacked, preferred_element_type=jnp.float32
-        ).astype(jnp.bfloat16)
+        product = jnp.dot(jnp.concatenate(live, axis=1), stacked, preferred_element_type=jnp.float32)
+        coupled[factor] = product.astype(jnp.bfloat16)
+
+    def beta(factor):
         for block in range(local_blocks):
-            source = coupled[:, block * tile_size : (block + 1) * tile_size]
+            source = coupled[factor, :, block * tile_size : (block + 1) * tile_size]
             tiles = [beta_tiles[factor, block, slot] for slot in range(beta_slots)]
             added = jnp.dot(source, jnp.concatenate(tiles, axis=1), preferred_element_type=jnp.float32)
             for slot in range(beta_slots):
@@ -78,10 +89,18 @@
                 away = (group ^ own_group) if by_xor else lax.rem(group - own_group + groups, groups)
                 place = away * local_blocks + lax.rem(target, local_blocks)
                 total[place] += added[:, slot * tile_size : (slot + 1) * tile_size]
-    for away in range(groups):
+
+    def both(factor, _):
+        alpha(factor)
+        beta(factor - 1)
+
+    alpha(0)
+    lax.fori_loop(1, factors, both, None, unroll=True)
+    beta(factors - 1)
+    for (away, first, last), out in zip(parts, outs):
         for block in range(local_blocks):
-            value = total[away * local_blocks + block].astype(jnp.bfloat16)
-            outs[away][:, block * tile_size : (block + 1) * tile_size] = value
+            value = total[away * local_blocks + block, first:last].astype(jnp.bfloat16)
+            out[:, block * tile_size : (block + 1) * tile_size] = value
 
 
 def shards(
@@ -93,36 +112,50 @@
     length, groups = lax.axis_size("alpha"), lax.axis_size("beta")
     held, place_of, _ = window_of(length)(ci_vector)
     by_xor = groups & (groups - 1) == 0
-    sizes = (factors, alpha_slots, local_blocks, beta_slots, groups, by_xor)
+    relay = groups == 4
+    direct = tile_size * 3 // 8 if relay else tile_size
+    parts = [(away, 0, tile_size if away < 2 else direct) for away in range(groups)]
+    if relay:
+        parts += [(away, direct, tile_size) for away in (2, 3)]
+    sizes = (factors, alpha_slots, local_blocks, beta_slots, groups, by_xor, parts)
     vmem = pl.BlockSpec(memory_space=pltpu.VMEM)
-    smem = pl.BlockSpec(memory_space=pltpu.SMEM)
     tile_bytes = (alpha_tiles.size + beta_tiles.size) * 2
 
-    counts = jnp.transpose(alpha_count, (1, 0))
-    counts = pl.pallas_call(
+    pl.pallas_call(
         warm_kernel,
-        out_shape=jax.ShapeDtypeStruct(counts.shape, counts.dtype),
-        in_specs=[vmem],
+        out_shape=jax.ShapeDtypeStruct((8, 128), jnp.float32),
         out_specs=vmem,
-        compiler_params=pltpu.CompilerParams(vmem_limit_bytes=2**20),
-        cost_estimate=pl.CostEstimate(flops=WARM_FLOPS, bytes_accessed=counts.size, transcendentals=0),
+        compiler_params=pltpu.CompilerParams(vmem_limit_bytes=2**20, has_side_effects=True),
+        cost_estimate=pl.CostEstimate(flops=WARM_FLOPS, bytes_accessed=4096, transcendentals=0),
         name="warm",
-    )(counts)
-
-    def body(sources, counts, targets, *refs):
-        n = len(held)
-        pieces = dict(zip(held, refs[:n]))
-        a_ref, b_ref, *outs = refs[n:-2]
-        couple_kernel(sizes, place_of, sources, counts, targets, pieces, a_ref, b_ref, outs, *refs[-2:])
+    )()
+
+    tables = [
+        jnp.transpose(alpha_list, (1, 2, 0)),
+        jnp.transpose(alpha_count, (1, 0)),
+        jnp.transpose(beta_target, (1, 2, 0)),
+    ]
+
+    def body(*refs):
+        t, n = len(tables), len(held)
+        pieces = dict(zip(held, refs[t : t + n]))
+        a_ref, b_ref, *outs = refs[t + n : t + n + 2 + len(parts)]
+        window, coupled, total, *near, semaphores = refs[t + n + 2 + len(parts) :]
+        couple_kernel(
+            sizes, place_of, refs[:t], pieces, a_ref, b_ref, outs, window, coupled, total, near, semaphores
+        )
 
     own, *far = pl.pallas_call(
         body,
-        out_shape=[jax.ShapeDtypeStruct((tile_size, columns), jnp.bfloat16)] * groups,
-        in_specs=[smem] * 3 + [vmem] * (len(held) + 2),
-        out_specs=[vmem] * groups,
+        out_shape=[jax.ShapeDtypeStruct((last - first, columns), jnp.bfloat16) for _, first, last in parts],
+        in_specs=[pl.BlockSpec(memory_space=pl.ANY)] * len(tables) + [vmem] * (len(held) + 2),
+        out_specs=[vmem] * len(parts),
         scratch_shapes=[
             pltpu.VMEM((max(held) + 1, tile_size, columns), jnp.bfloat16),
+            pltpu.VMEM((factors, tile_size, columns), jnp.bfloat16),
             pltpu.VMEM((groups * local_blocks, tile_size, tile_size), jnp.float32),
+            *[pltpu.SMEM(table.shape, jnp.int32) for table in tables],
+            pltpu.SemaphoreType.DMA((len(tables),)),
         ],
         compiler_params=pltpu.CompilerParams(vmem_limit_bytes=20 * 2**20),
         cost_estimate=pl.CostEstimate(
@@ -132,26 +165,27 @@
         ),
         name="couple",
     )(
-        jnp.transpose(alpha_list, (1, 2, 0)),
-        counts,
-        jnp.transpose(beta_target, (1, 2, 0)),
+        *tables,
         *held.values(),
         alpha_tiles,
         beta_tiles,
     )
-    summed = own.astype(jnp.float32)
-    for away in far_order(groups):
+
+    def send(value, away):
         if by_xor:
             pairs = [(i, i ^ away) for i in range(groups)]
         else:
             pairs = [(i, (i + away) % groups) for i in range(groups)]
-        received = lax.ppermute(far[away - 1], "beta", pairs)
-        summed = summed + received.astype(jnp.float32)
+        return lax.ppermute(value, "beta", pairs)
+
+    received = [send(far[away - 1], away).astype(jnp.float32) for away in range(1, groups)]
+    if relay:
+        beyond = send(far[-1], 1)
+        joined = (far[-2].astype(jnp.float32) + beyond.astype(jnp.float32)).astype(jnp.bfloat16)
+        passed = send(joined, 2).astype(jnp.float32)
+        received[1:] = [jnp.concatenate([received[1] + received[2], passed], axis=0)]
+    summed = own.astype(jnp.float32) + sum(received)
     return summed + (alpha_diag[:, None] + beta_diag[None, :]) * ci_vector.astype(jnp.float32)
-
-
-def far_order(groups):
-    return [*range(2, groups), *range(1, min(groups, 2))]
 
 
 def window_of(length):

time: 32.5 us -> 35.3 us (1.086)
  waiting for transfers between devices: 14 us -> 8.68 us
  starting transfers between devices: 11.2 us -> 15.7 us
  local copies, waits for them, and re-layouts: 2.48 us -> 6.36 us
    ppermute x3 -> x5, waiting for transfers between devices: 9.67 us -> 3.62 us  [send(): return lax.ppermute(value, 'beta', pairs)]
    ppermute x3 -> x5, starting transfers between devices: 4.21 us -> 8.69 us  [send(): return lax.ppermute(value, 'beta', pairs)]
    unnamed x16, local copies, waits for them, and re-layouts: 2.48 us -> 6.36 us
    ppermute x2, waiting for transfers between devices: 0.6 us -> 1.33 us  [cube_window(): held[k + 1] = lax.ppermute(held[k], 'alpha', swap)]
  transfers between devices with their start and end apart: 9 -> 11, of which waited for: 4 -> 5; matrix products, arithmetic and copies ran while one was open for 0% -> 0% of each run, Pallas kernels for 0% -> 2%
where the time goes in v1:
time: 35.3 us; the launch traced here: 35 us
  starting transfers between devices  15.7 us (44%)
  waiting for transfers between devices  8.68 us (25%)
  local copies, waits for them, and re-layouts  6.36 us (18%)
  Pallas kernels  3.37 us (10%)
  other arithmetic  0.85 us (2%)
    ppermute x5, starting transfers between devices, send(): return lax.ppermute(value, 'beta', pairs)  8.69 us
    unnamed x16, local copies, waits for them, and re-layouts  6.36 us
    ppermute x2, starting transfers between devices, cube_window(): held[k] = lax.ppermute(ci_vector, 'alpha', pairs)  4.46 us
    ppermute x2, waiting for transfers between devices, cube_window(): held[k] = lax.ppermute(ci_vector, 'alpha', pairs)  3.73 us
    ppermute x5, waiting for transfers between devices, send(): return lax.ppermute(value, 'beta', pairs)  3.62 us
    pallas_call x1, Pallas kernels, shards(): pl.pallas_call(body, out_shape=[jax.ShapeDtypeStruct((last - first, colum...  2.78 us
    ppermute x1, starting transfers between devices, cube_window(): held[k + 1] = lax.ppermute(ci_vector, 'alpha', pairs)  1.55 us
    ppermute x2, waiting for transfers between devices, cube_window(): held[k + 1] = lax.ppermute(held[k], 'alpha', swap)  1.33 us
  transfers between devices with their start and end apart: 11, of which 5 were waited for; matrix products, arithmetic and copies ran while one was open for 0% of the time, Pallas kernels for 2%

profile of v1, /device:TPU:0, one launch (start us, length us, event | category | flops | bytes accessed | tf_op | source)
XLA Modules:
  0.0 35.0 jit_solution(13419621226141748392)
XLA Ops:
  0.0 0.5 %collective-permute-start.2 = (bf16[128,512]{1,0:T(8,128)(2,1)}, bf16[128,512]{1,0:T(8,128)(2,1)S(1)}, u32[]{:S(2)}, u32[]{:S(2)}) collective-permute-start(bf16[128,512]{1,0:T(8,128)(2,1)} %refs_3_.1), channel_id=1, source_target_pairs={{4,0},{0,4},{16,8},{20,12},{8,16},{12,20},{28,24},{24,28},{5,1},{1... | collective-permute-start | bytes 393224 | tf_op jit(solution)/shard_map/ppermute | solution.py:36
  0.5 4.0 %collective-permute-start = (bf16[128,512]{1,0:T(8,128)(2,1)}, bf16[128,512]{1,0:T(8,128)(2,1)S(1)}, u32[]{:S(2)}, u32[]{:S(2)}) collective-permute-start(bf16[128,512]{1,0:T(8,128)(2,1)} %refs_3_.1), channel_id=1, source_target_pairs={{8,0},{12,4},{0,8},{4,12},{24,16},{28,20},{16,24},{20,28},{9,1},{1... | collective-permute-start | bytes 393224 | tf_op jit(solution)/shard_map/ppermute | solution.py:36
  4.5 0.0 collective-permute-start.3
  4.5 1.6 %collective-permute-start.1 = (bf16[128,512]{1,0:T(8,128)(2,1)}, bf16[128,512]{1,0:T(8,128)(2,1)S(1)}, u32[]{:S(2)}, u32[]{:S(2)}) collective-permute-start(bf16[128,512]{1,0:T(8,128)(2,1)} %refs_3_.1), channel_id=1, source_target_pairs={{0,0},{16,4},{8,8},{24,12},{4,16},{20,20},{12,24},{28,28},{1,1},{1... | collective-permute-start | bytes 393224 | tf_op jit(solution)/shard_map/ppermute | solution.py:41
  6.0 0.0 collective-permute-done.2.refs_6_
  6.0 0.9 %collective-permute-start.5 = (bf16[128,512]{1,0:T(8,128)(2,1)S(1)}, bf16[128,512]{1,0:T(8,128)(2,1)S(1)}, u32[]{:S(2)}, u32[]{:S(2)}) collective-permute-start(bf16[128,512]{1,0:T(8,128)(2,1)S(1)} %collective-permute-done.2.refs_6_), channel_id=1, source_target_pairs={{0,4},{4,0},{8,12},{12,8},{16,20},{20,16},{24,28},{28,24},{1,5},{5... | collective-permute-start | bytes 393224 | tf_op jit(solution)/shard_map/ppermute | solution.py:45
  7.0 3.7 %collective-permute-done.refs_4_ = bf16[128,512]{1,0:T(8,128)(2,1)S(1)} collective-permute-done((bf16[128,512]{1,0:T(8,128)(2,1)}, bf16[128,512]{1,0:T(8,128)(2,1)S(1)}, u32[]{:S(2)}, u32[]{:S(2)}) %collective-permute-start) | collective-permute-done | bytes 131104 | tf_op jit(solution)/shard_map/ppermute | solution.py:36
  10.7 0.0 collective-permute-start.4
  10.7 0.0 collective-permute-done.3.refs_7_
  10.7 0.0 collective-permute-done.1.refs_5_
  10.7 0.0 collective-permute-done.5.refs_9_
  10.7 1.3 %collective-permute-done.4.refs_8_ = bf16[128,512]{1,0:T(8,128)(2,1)S(1)} collective-permute-done((bf16[128,512]{1,0:T(8,128)(2,1)S(1)}, bf16[128,512]{1,0:T(8,128)(2,1)S(1)}, u32[]{:S(2)}, u32[]{:S(2)}) %collective-permute-start.4) | collective-permute-done | bytes 131104 | tf_op jit(solution)/shard_map/ppermute | solution.py:45
  12.0 0.0 copy-start
  12.0 2.2 %copy-done = bf16[8,4,4,128,128]{4,3,2,1,0:T(8,128)(2,1)S(1)} copy-done((bf16[8,4,4,128,128]{4,3,2,1,0:T(8,128)(2,1)S(1)}, bf16[8,4,4,128,128]{4,3,2,1,0:T(8,128)(2,1)}, u32[]{:S(2)}) %copy-start) | copy-done | bytes 4194328
  14.2 0.0 copy-start.1
  14.2 1.2 %copy-done.1 = bf16[8,1,4,128,128]{4,3,2,1,0:T(8,128)(2,1)S(1)} copy-done((bf16[8,1,4,128,128]{4,3,2,1,0:T(8,128)(2,1)S(1)}, bf16[8,1,4,128,128]{4,3,2,1,0:T(8,128)(2,1)}, u32[]{:S(2)}) %copy-start.1) | copy-done | bytes 1048600
  15.5 0.0 copy-start.2
  15.5 0.9 %copy-done.2 = bf16[128,512]{1,0:T(8,128)(2,1)S(1)} copy-done((bf16[128,512]{1,0:T(8,128)(2,1)S(1)}, bf16[128,512]{1,0:T(8,128)(2,1)}, u32[]{:S(2)}) %copy-start.2) | copy-done | bytes 131096
  16.4 0.0 copy-start.3
  16.4 0.7 %copy-done.3 = s32[8,4,4]{0,2,1:T(4,128)S(1)} copy-done((s32[8,4,4]{0,2,1:T(4,128)S(1)}, s32[8,4,4]{0,2,1:T(4,128)}, u32[]{:S(2)}) %copy-start.3) | copy-done | bytes 536
  17.1 0.0 copy-start.4
  17.1 0.7 %copy-done.4 = s32[8,1,4]{0,2,1:T(4,128)S(1)} copy-done((s32[8,1,4]{0,2,1:T(4,128)S(1)}, s32[8,1,4]{0,2,1:T(4,128)}, u32[]{:S(2)}) %copy-start.4) | copy-done | bytes 152
  17.7 0.0 copy-start.5
  17.7 0.7 %copy-done.5 = s32[8,1]{0,1:T(1,128)S(1)} copy-done((s32[8,1]{0,1:T(1,128)S(1)}, s32[8,1]{0,1:T(1,128)}, u32[]{:S(2)}) %copy-start.5) | copy-done | bytes 56
  18.4 2.8 %couple.1 = (bf16[128,512]{1,0:T(8,128)(2,1)S(1)}, bf16[128,512]{1,0:T(8,128)(2,1)S(1)}, bf16[48,512]{1,0:T(8,128)(2,1)S(1)}, bf16[48,512]{1,0:T(8,128)(2,1)S(1)...) custom-call(s32[1,4,8]{2,1,0:T(4,128)S(1)} %bitcast.4, s32[1,8]{1,0:T(1,128)S(1)} %bitcast.5, ...), custom_call_target="tpu_custom_call" | custom-call | flops 1073741824 | bytes 5242880 | tf_op jit(solution)/shard_map/couple/pallas_call | solution.py:148
  21.2 0.0 copy-start.6
  21.2 0.0 copy-start.7
  21.2 1.6 %collective-permute-start.9 = (bf16[80,512]{1,0:T(8,128)(2,1)S(1)}, bf16[80,512]{1,0:T(8,128)(2,1)S(1)}, u32[]{:S(2)}, u32[]{:S(2)}) collective-permute-start(bf16[80,512]{1,0:T(8,128)(2,1)S(1)} %get-tuple-element.16), channel_id=1, source_target_pairs={{0,1},{1,0},{2,3},{3,2},{4,5},{5,4},{6,7},{7,6},{8,9},{9,8},{10,11... | collective-permute-start | bytes 245768 | tf_op jit(solution)/shard_map/ppermute | solution.py:179
  22.8 0.6 %warm.1 = f32[8,128]{1,0:T(8,128)} custom-call(), custom_call_target="tpu_custom_call" | custom-call | flops 20000000000 | bytes 4096 | tf_op jit(solution)/shard_map/warm/pallas_call | solution.py:124
  23.4 2.6 %collective-permute-start.7 = (bf16[48,512]{1,0:T(8,128)(2,1)S(1)}, bf16[48,512]{1,0:T(8,128)(2,1)S(1)}, u32[]{:S(2)}, u32[]{:S(2)}) collective-permute-start(bf16[48,512]{1,0:T(8,128)(2,1)S(1)} %get-tuple-element.13), channel_id=1, source_target_pairs={{0,2},{1,3},{2,0},{3,1},{4,6},{5,7},{6,4},{7,5},{8,10},{9,11},{10,... | collective-permute-start | bytes 147464 | tf_op jit(solution)/shard_map/ppermute | solution.py:179
  26.0 0.2 collective-permute-start.8
  26.3 0.7 %collective-permute-start.6 = (bf16[128,512]{1,0:T(8,128)(2,1)S(1)}, bf16[128,512]{1,0:T(8,128)(2,1)S(1)}, u32[]{:S(2)}, u32[]{:S(2)}) collective-permute-start(bf16[128,512]{1,0:T(8,128)(2,1)S(1)} %get-tuple-element.12), channel_id=1, source_target_pairs={{0,1},{1,0},{2,3},{3,2},{4,5},{5,4},{6,7},{7,6},{8,9},{9,8},{10,11... | collective-permute-start | bytes 393224 | tf_op jit(solution)/shard_map/ppermute | solution.py:179
  26.9 0.0 collective-permute-done.9
  27.0 3.6 %collective-permute-start.10 = (bf16[80,512]{1,0:T(8,128)(2,1)S(1)}, bf16[80,512]{1,0:T(8,128)(2,1)S(1)}, u32[]{:S(2)}, u32[]{:S(2)}) collective-permute-start(bf16[80,512]{1,0:T(8,128)(2,1)S(1)} %add_convert_fusion), channel_id=1, source_target_pairs={{0,2},{1,3},{2,0},{3,1},{4,6},{5,7},{6,4},{7,5},{8,10},{9,11},{10,... | collective-permute-start | bytes 245768 | tf_op jit(solution)/shard_map/ppermute | solution.py:179
  30.5 0.0 collective-permute-done.7
  30.5 1.9 %collective-permute-done.8 = bf16[48,512]{1,0:T(8,128)(2,1)S(1)} collective-permute-done((bf16[48,512]{1,0:T(8,128)(2,1)S(1)}, bf16[48,512]{1,0:T(8,128)(2,1)S(1)}, u32[]{:S(2)}, u32[]{:S(2)}) %collective-permute-start.8) | collective-permute-done | bytes 49184 | tf_op jit(solution)/shard_map/ppermute | solution.py:179
  32.5 1.3 %collective-permute-done.10 = bf16[80,512]{1,0:T(8,128)(2,1)S(1)} collective-permute-done((bf16[80,512]{1,0:T(8,128)(2,1)S(1)}, bf16[80,512]{1,0:T(8,128)(2,1)S(1)}, u32[]{:S(2)}, u32[]{:S(2)}) %collective-permute-start.10) | collective-permute-done | bytes 81952 | tf_op jit(solution)/shard_map/ppermute | solution.py:179
  33.8 0.4 %collective-permute-done.6 = bf16[128,512]{1,0:T(8,128)(2,1)S(1)} collective-permute-done((bf16[128,512]{1,0:T(8,128)(2,1)S(1)}, bf16[128,512]{1,0:T(8,128)(2,1)S(1)}, u32[]{:S(2)}, u32[]{:S(2)}) %collective-permute-start.6) | collective-permute-done | bytes 131104 | tf_op jit(solution)/shard_map/ppermute | solution.py:179
  34.2 0.0 copy-done.6
  34.2 0.0 copy-done.7
  34.2 0.8 %fusion.1 = f32[128,512]{1,0:T(8,128)} fusion(f32[80,512]{1,0:T(8,128)S(1)} %convert_element_type.34, f32[48,512]{1,0:T(8,128)S(1)} %convert_add_fusion, bf16[128,512]{1,0:T(8,128)(2,1)S(1)} %copy-done.2, bf16[128,512]{1,0:T(8,128)(2,1)S(1)} %collective-permute-done.6, bf16[128,512]{1,0:T(8,128)(2,1)S(1)} %get-tuple-element.11, f32[512]{0:T(512)S(1)} %copy-done.6, ...), kind=kLoop, calls=%fused_computation.2 | loop fusion | flops 589824 | bytes 920064 | tf_op jit(solution)/shard_map/add | solution.py:188
  (3 shorter events, 0.0 us)
Async XLA Ops:
  0.0 6.0 %collective-permute-start.2 = (bf16[128,512]{1,0:T(8,128)(2,1)}, bf16[128,512]{1,0:T(8,128)(2,1)S(1)}, u32[]{:S(2)}, u32[]{:S(2)}) collective-permute-start(bf16[128,512]{1,0:T(8,128)(2,1)} %refs_3_.1), channel_id=1, source_target_pairs={{4,0},{0,4},{16,8},{20,12},{8,16},{12,20},{28,24},{24,28},{5,1},{1... | collective-permute-start | bytes 393224 | tf_op jit(solution)/shard_map/ppermute | solution.py:36
  0.5 10.2 %collective-permute-start = (bf16[128,512]{1,0:T(8,128)(2,1)}, bf16[128,512]{1,0:T(8,128)(2,1)S(1)}, u32[]{:S(2)}, u32[]{:S(2)}) collective-permute-start(bf16[128,512]{1,0:T(8,128)(2,1)} %refs_3_.1), channel_id=1, source_target_pairs={{8,0},{12,4},{0,8},{4,12},{24,16},{28,20},{16,24},{20,28},{9,1},{1... | collective-permute-start | bytes 393224 | tf_op jit(solution)/shard_map/ppermute | solution.py:36
  4.5 6.2 %collective-permute-start.3 = (bf16[128,512]{1,0:T(8,128)(2,1)}, bf16[128,512]{1,0:T(8,128)(2,1)S(1)}, u32[]{:S(2)}, u32[]{:S(2)}) collective-permute-start(bf16[128,512]{1,0:T(8,128)(2,1)} %refs_3_.1), channel_id=1, source_target_pairs={{0,4},{4,0},{8,12},{12,8},{16,20},{20,16},{24,28},{28,24},{1,5},{5... | collective-permute-start | bytes 393224 | tf_op jit(solution)/shard_map/ppermute | solution.py:43
  4.5 6.2 %collective-permute-start.1 = (bf16[128,512]{1,0:T(8,128)(2,1)}, bf16[128,512]{1,0:T(8,128)(2,1)S(1)}, u32[]{:S(2)}, u32[]{:S(2)}) collective-permute-start(bf16[128,512]{1,0:T(8,128)(2,1)} %refs_3_.1), channel_id=1, source_target_pairs={{0,0},{16,4},{8,8},{24,12},{4,16},{20,20},{12,24},{28,28},{1,1},{1... | collective-permute-start | bytes 393224 | tf_op jit(solution)/shard_map/ppermute | solution.py:41
  6.0 4.7 %collective-permute-start.5 = (bf16[128,512]{1,0:T(8,128)(2,1)S(1)}, bf16[128,512]{1,0:T(8,128)(2,1)S(1)}, u32[]{:S(2)}, u32[]{:S(2)}) collective-permute-start(bf16[128,512]{1,0:T(8,128)(2,1)S(1)} %collective-permute-done.2.refs_6_), channel_id=1, source_target_pairs={{0,4},{4,0},{8,12},{12,8},{16,20},{20,16},{24,28},{28,24},{1,5},{5... | collective-permute-start | bytes 393224 | tf_op jit(solution)/shard_map/ppermute | solution.py:45
  10.7 1.3 %collective-permute-start.4 = (bf16[128,512]{1,0:T(8,128)(2,1)S(1)}, bf16[128,512]{1,0:T(8,128)(2,1)S(1)}, u32[]{:S(2)}, u32[]{:S(2)}) collective-permute-start(bf16[128,512]{1,0:T(8,128)(2,1)S(1)} %collective-permute-done.refs_4_), channel_id=1, source_target_pairs={{0,4},{4,0},{8,12},{12,8},{16,20},{20,16},{24,28},{28,24},{1,5},{5... | collective-permute-start | bytes 393224 | tf_op jit(solution)/shard_map/ppermute | solution.py:45
  12.0 2.2 %copy-start = (bf16[8,4,4,128,128]{4,3,2,1,0:T(8,128)(2,1)S(1)}, bf16[8,4,4,128,128]{4,3,2,1,0:T(8,128)(2,1)}, u32[]{:S(2)}) copy-start(bf16[8,4,4,128,128]{4,3,2,1,0:T(8,128)(2,1)} %refs_11_.1) | copy-start | bytes 12582916
  14.2 1.2 %copy-start.1 = (bf16[8,1,4,128,128]{4,3,2,1,0:T(8,128)(2,1)S(1)}, bf16[8,1,4,128,128]{4,3,2,1,0:T(8,128)(2,1)}, u32[]{:S(2)}) copy-start(bf16[8,1,4,128,128]{4,3,2,1,0:T(8,128)(2,1)} %refs_10_.1) | copy-start | bytes 3145732
  15.5 0.9 %copy-start.2 = (bf16[128,512]{1,0:T(8,128)(2,1)S(1)}, bf16[128,512]{1,0:T(8,128)(2,1)}, u32[]{:S(2)}) copy-start(bf16[128,512]{1,0:T(8,128)(2,1)} %refs_3_.1) | copy-start | bytes 393220
  16.4 0.7 %copy-start.3 = (s32[8,4,4]{0,2,1:T(4,128)S(1)}, s32[8,4,4]{0,2,1:T(4,128)}, u32[]{:S(2)}) copy-start(s32[8,4,4]{0,2,1:T(4,128)} %param.13) | copy-start | bytes 1540
  17.1 0.7 %copy-start.4 = (s32[8,1,4]{0,2,1:T(4,128)S(1)}, s32[8,1,4]{0,2,1:T(4,128)}, u32[]{:S(2)}) copy-start(s32[8,1,4]{0,2,1:T(4,128)} %param.10) | copy-start | bytes 388
  17.7 0.7 %copy-start.5 = (s32[8,1]{0,1:T(1,128)S(1)}, s32[8,1]{0,1:T(1,128)}, u32[]{:S(2)}) copy-start(s32[8,1]{0,1:T(1,128)} %param.11) | copy-start | bytes 100
  21.2 13.0 %copy-start.6 = (f32[512]{0:T(512)S(1)}, f32[512]{0:T(512)}, u32[]{:S(2)}) copy-start(f32[512]{0:T(512)} %param.15) | copy-start | bytes 6148
  21.2 13.0 %copy-start.7 = (f32[128]{0:T(128)S(1)}, f32[128]{0:T(128)}, u32[]{:S(2)}) copy-start(f32[128]{0:T(128)} %param.14) | copy-start | bytes 1540
  21.2 5.7 %collective-permute-start.9 = (bf16[80,512]{1,0:T(8,128)(2,1)S(1)}, bf16[80,512]{1,0:T(8,128)(2,1)S(1)}, u32[]{:S(2)}, u32[]{:S(2)}) collective-permute-start(bf16[80,512]{1,0:T(8,128)(2,1)S(1)} %get-tuple-element.16), channel_id=1, source_target_pairs={{0,1},{1,0},{2,3},{3,2},{4,5},{5,4},{6,7},{7,6},{8,9},{9,8},{10,11... | collective-permute-start | bytes 245768 | tf_op jit(solution)/shard_map/ppermute | solution.py:179
  23.4 7.1 %collective-permute-start.7 = (bf16[48,512]{1,0:T(8,128)(2,1)S(1)}, bf16[48,512]{1,0:T(8,128)(2,1)S(1)}, u32[]{:S(2)}, u32[]{:S(2)}) collective-permute-start(bf16[48,512]{1,0:T(8,128)(2,1)S(1)} %get-tuple-element.13), channel_id=1, source_target_pairs={{0,2},{1,3},{2,0},{3,1},{4,6},{5,7},{6,4},{7,5},{8,10},{9,11},{10,... | collective-permute-start | bytes 147464 | tf_op jit(solution)/shard_map/ppermute | solution.py:179
  26.0 6.4 %collective-permute-start.8 = (bf16[48,512]{1,0:T(8,128)(2,1)S(1)}, bf16[48,512]{1,0:T(8,128)(2,1)S(1)}, u32[]{:S(2)}, u32[]{:S(2)}) collective-permute-start(bf16[48,512]{1,0:T(8,128)(2,1)S(1)} %get-tuple-element.14), channel_id=1, source_target_pairs={{0,3},{1,2},{2,1},{3,0},{4,7},{5,6},{6,5},{7,4},{8,11},{9,10},{10,... | collective-permute-start | bytes 147464 | tf_op jit(solution)/shard_map/ppermute | solution.py:179
  26.3 7.9 %collective-permute-start.6 = (bf16[128,512]{1,0:T(8,128)(2,1)S(1)}, bf16[128,512]{1,0:T(8,128)(2,1)S(1)}, u32[]{:S(2)}, u32[]{:S(2)}) collective-permute-start(bf16[128,512]{1,0:T(8,128)(2,1)S(1)} %get-tuple-element.12), channel_id=1, source_target_pairs={{0,1},{1,0},{2,3},{3,2},{4,5},{5,4},{6,7},{7,6},{8,9},{9,8},{10,11... | collective-permute-start | bytes 393224 | tf_op jit(solution)/shard_map/ppermute | solution.py:179
  27.0 6.8 %collective-permute-start.10 = (bf16[80,512]{1,0:T(8,128)(2,1)S(1)}, bf16[80,512]{1,0:T(8,128)(2,1)S(1)}, u32[]{:S(2)}, u32[]{:S(2)}) collective-permute-start(bf16[80,512]{1,0:T(8,128)(2,1)S(1)} %add_convert_fusion), channel_id=1, source_target_pairs={{0,2},{1,3},{2,0},{3,1},{4,6},{5,7},{6,4},{7,5},{8,10},{9,11},{10,... | collective-permute-start | bytes 245768 | tf_op jit(solution)/shard_map/ppermute | solution.py:179

commit v2 on v1

--- a/solution.py
+++ b/solution.py
@@ -22,28 +22,44 @@
 
 def cube_window(ci_vector):
     length = lax.axis_size("alpha")
-
-    def near(i, source):
-        return abs(i - source) <= BAND
-
-    held, relayed = {0: ci_vector}, []
-    for k in range(2, length, 2):
-        even = [i for i in range(length) if near(i, i ^ k)]
-        odd = [i for i in range(length) if near(i, i ^ k ^ 1)]
-        if even:
-            taking = {i for i in range(length) if near(i, i ^ k) or near(i ^ 1, i ^ k)}
-            pairs = [(i ^ (k if i in taking else 1), i) for i in range(length)]
-            held[k] = lax.ppermute(ci_vector, "alpha", pairs)
-            if odd:
-                relayed.append(k)
-        elif odd:
-            pairs = [(i ^ (k ^ 1 if i in odd else 0), i) for i in range(length)]
-            held[k + 1] = lax.ppermute(ci_vector, "alpha", pairs)
-    swap = [(i, i ^ 1) for i in range(length)]
-    held[1] = lax.ppermute(ci_vector, "alpha", swap)
-    for k in relayed:
-        held[k + 1] = lax.ppermute(held[k], "alpha", swap)
-    return held, lambda block, own: block ^ own, ()
+    everyone = range(length)
+    lower, middle = set(everyone[: length // 2]), set(everyone[length // 4 : -(length // 4)])
+    first = lax.ppermute(ci_vector, "alpha", [(i ^ (2 if i in lower else 1), i) for i in everyone])
+    cross = lax.ppermute(ci_vector, "alpha", [(i ^ (6 if i in middle else 1), i) for i in everyone])
+    last = lax.ppermute(ci_vector, "alpha", [(i ^ (1 if i in lower else 2), i) for i in everyone])
+    edge = lax.ppermute(ci_vector, "alpha", [(i ^ 5, i) for i in everyone if abs(i - (i ^ 5)) <= BAND])
+    swap = [(i, i ^ 1) for i in everyone]
+    beside = pl.pallas_call(
+        pick_kernel,
+        out_shape=jax.ShapeDtypeStruct(ci_vector.shape, ci_vector.dtype),
+        in_specs=[pl.BlockSpec(memory_space=pltpu.VMEM)] * 2,
+        out_specs=pl.BlockSpec(memory_space=pltpu.VMEM),
+        compiler_params=pltpu.CompilerParams(vmem_limit_bytes=2**20),
+        cost_estimate=pl.CostEstimate(flops=10**6, bytes_accessed=4 * ci_vector.size, transcendentals=0),
+        name="pick",
+    )(first, last)
+    held = {0: ci_vector, 1: last, 2: first, 5: edge, 6: cross}
+    held[3] = lax.ppermute(beside, "alpha", swap)
+    held[7] = lax.ppermute(cross, "alpha", swap)
+
+    def place_of(block, own):
+        k = block ^ own
+        turned = (own >= length // 2) & ((k == 1) | (k == 2))
+        return jnp.where(turned, 3 - k, k)
+
+    return held, place_of, ()
+
+
+def pick_kernel(first, last, out):
+    lower = lax.axis_index("alpha") < lax.axis_size("alpha") // 2
+
+    @pl.when(lower)
+    def _():
+        out[...] = first[...]
+
+    @pl.when(jnp.logical_not(lower))
+    def _():
+        out[...] = last[...]
 
 
 def warm_kernel(out):
@@ -189,7 +205,7 @@
 
 
 def window_of(length):
-    return cube_window if length & (length - 1) == 0 and length <= 2 * (BAND + 1) else band_window
+    return cube_window if length == 2 * (BAND + 1) else band_window
 
 
 def solution(mesh):

time: 35.3 us -> 35.4 us (level)
  no operation moved by 1% of the time
where the time goes in v2:
time: 35.4 us; the launch traced here: 35.1 us
  starting transfers between devices  15.8 us (45%)
  waiting for transfers between devices  8.54 us (24%)
  local copies, waits for them, and re-layouts  6.36 us (18%)
  Pallas kernels  3.4 us (10%)
  other arithmetic  0.85 us (2%)
    ppermute x5, starting transfers between devices, send(): return lax.ppermute(value, 'beta', pairs)  8.68 us
    unnamed x16, local copies, waits for them, and re-layouts  6.36 us
    ppermute x1, starting transfers between devices, cube_window(): lax.ppermute(ci_vector, 'alpha', [(i ^ (2 if i in lower else 1), i) for i...  3.97 us
    ppermute x5, waiting for transfers between devices, send(): return lax.ppermute(value, 'beta', pairs)  3.62 us
    ppermute x1, waiting for transfers between devices, cube_window(): lax.ppermute(ci_vector, 'alpha', [(i ^ (2 if i in lower else 1), i) for i...  3.59 us
    pallas_call x1, Pallas kernels, shards(): pl.pallas_call(body, out_shape=[jax.ShapeDtypeStruct((last - first, colum...  2.79 us
    ppermute x1, starting transfers between devices, cube_window(): held[7] = lax.ppermute(cross, 'alpha', swap)  1.96 us
    ppermute x1, waiting for transfers between devices, cube_window(): held[3] = lax.ppermute(beside, 'alpha', swap)  1.31 us
  transfers between devices with their start and end apart: 11, of which 5 were waited for; matrix products, arithmetic and copies ran while one was open for 0% of the time, Pallas kernels for 2%

profile of v2, /device:TPU:0, one launch (start us, length us, event | category | flops | bytes accessed | tf_op | source)
XLA Modules:
  0.0 35.1 jit_solution(3085471768271974932)
XLA Ops:
  0.0 0.5 %collective-permute-start.3 = (bf16[128,512]{1,0:T(8,128)(2,1)}, bf16[128,512]{1,0:T(8,128)(2,1)S(1)}, u32[]{:S(2)}, u32[]{:S(2)}) collective-permute-start(bf16[128,512]{1,0:T(8,128)(2,1)} %refs_3_.1), channel_id=1, source_target_pairs={{4,0},{0,4},{16,8},{20,12},{8,16},{12,20},{28,24},{24,28},{5,1},{1... | collective-permute-start | bytes 393224 | tf_op jit(solution)/shard_map/ppermute | solution.py:28
  0.5 4.0 %collective-permute-start.1 = (bf16[128,512]{1,0:T(8,128)(2,1)}, bf16[128,512]{1,0:T(8,128)(2,1)S(1)}, u32[]{:S(2)}, u32[]{:S(2)}) collective-permute-start(bf16[128,512]{1,0:T(8,128)(2,1)} %refs_3_.1), channel_id=1, source_target_pairs={{8,0},{12,4},{0,8},{4,12},{20,16},{16,20},{28,24},{24,28},{9,1},{1... | collective-permute-start | bytes 393224 | tf_op jit(solution)/shard_map/ppermute | solution.py:27
  4.5 0.0 collective-permute-start
  4.5 0.7 %collective-permute-start.2 = (bf16[128,512]{1,0:T(8,128)(2,1)}, bf16[128,512]{1,0:T(8,128)(2,1)S(1)}, u32[]{:S(2)}, u32[]{:S(2)}) collective-permute-start(bf16[128,512]{1,0:T(8,128)(2,1)} %refs_3_.1), channel_id=1, source_target_pairs={{16,4},{24,12},{4,16},{12,24},{17,5},{25,13},{5,17},{13,25},{18,6}... | collective-permute-start | bytes 393224 | tf_op jit(solution)/shard_map/ppermute | solution.py:30
  5.1 0.0 collective-permute-done.3.refs_7_
  5.1 2.0 %collective-permute-start.5 = (bf16[128,512]{1,0:T(8,128)(2,1)S(1)}, bf16[128,512]{1,0:T(8,128)(2,1)S(1)}, u32[]{:S(2)}, u32[]{:S(2)}) collective-permute-start(bf16[128,512]{1,0:T(8,128)(2,1)S(1)} %collective-permute-done.3.refs_7_), channel_id=1, source_target_pairs={{0,4},{4,0},{8,12},{12,8},{16,20},{20,16},{24,28},{28,24},{1,5},{5... | collective-permute-start | bytes 393224 | tf_op jit(solution)/shard_map/ppermute | solution.py:43
  7.1 3.6 %collective-permute-done.1.first.refs_5_ = bf16[128,512]{1,0:T(8,128)(2,1)S(1)} collective-permute-done((bf16[128,512]{1,0:T(8,128)(2,1)}, bf16[128,512]{1,0:T(8,128)(2,1)S(1)}, u32[]{:S(2)}, u32[]{:S(2)}) %collective-permute-start.1) | collective-permute-done | bytes 131104 | tf_op jit(solution)/shard_map/ppermute | solution.py:27
  10.7 0.0 collective-permute-done.last.refs_4_
  10.7 0.1 collective-permute-start.4
  10.8 0.0 collective-permute-done.2.refs_6_
  10.8 0.0 collective-permute-done.5.refs_9_
  10.8 1.3 %collective-permute-done.4.refs_8_ = bf16[128,512]{1,0:T(8,128)(2,1)S(1)} collective-permute-done((bf16[128,512]{1,0:T(8,128)(2,1)S(1)}, bf16[128,512]{1,0:T(8,128)(2,1)S(1)}, u32[]{:S(2)}, u32[]{:S(2)}) %collective-permute-start.4) | collective-permute-done | bytes 131104 | tf_op jit(solution)/shard_map/ppermute | solution.py:42
  12.1 0.0 copy-start
  12.1 2.2 %copy-done = bf16[8,4,4,128,128]{4,3,2,1,0:T(8,128)(2,1)S(1)} copy-done((bf16[8,4,4,128,128]{4,3,2,1,0:T(8,128)(2,1)S(1)}, bf16[8,4,4,128,128]{4,3,2,1,0:T(8,128)(2,1)}, u32[]{:S(2)}) %copy-start) | copy-done | bytes 4194328
  14.3 0.0 copy-start.1
  14.3 1.2 %copy-done.1 = bf16[8,1,4,128,128]{4,3,2,1,0:T(8,128)(2,1)S(1)} copy-done((bf16[8,1,4,128,128]{4,3,2,1,0:T(8,128)(2,1)S(1)}, bf16[8,1,4,128,128]{4,3,2,1,0:T(8,128)(2,1)}, u32[]{:S(2)}) %copy-start.1) | copy-done | bytes 1048600
  15.5 0.0 copy-start.2
  15.5 0.9 %copy-done.2 = bf16[128,512]{1,0:T(8,128)(2,1)S(1)} copy-done((bf16[128,512]{1,0:T(8,128)(2,1)S(1)}, bf16[128,512]{1,0:T(8,128)(2,1)}, u32[]{:S(2)}) %copy-start.2) | copy-done | bytes 131096
  16.4 0.0 copy-start.3
  16.4 0.7 %copy-done.3 = s32[8,4,4]{0,2,1:T(4,128)S(1)} copy-done((s32[8,4,4]{0,2,1:T(4,128)S(1)}, s32[8,4,4]{0,2,1:T(4,128)}, u32[]{:S(2)}) %copy-start.3) | copy-done | bytes 536
  17.1 0.0 copy-start.4
  17.1 0.7 %copy-done.4 = s32[8,1,4]{0,2,1:T(4,128)S(1)} copy-done((s32[8,1,4]{0,2,1:T(4,128)S(1)}, s32[8,1,4]{0,2,1:T(4,128)}, u32[]{:S(2)}) %copy-start.4) | copy-done | bytes 152
  17.8 0.0 copy-start.5
  17.8 0.7 %copy-done.5 = s32[8,1]{0,1:T(1,128)S(1)} copy-done((s32[8,1]{0,1:T(1,128)S(1)}, s32[8,1]{0,1:T(1,128)}, u32[]{:S(2)}) %copy-start.5) | copy-done | bytes 56
  18.5 2.8 %couple.1 = (bf16[128,512]{1,0:T(8,128)(2,1)S(1)}, bf16[128,512]{1,0:T(8,128)(2,1)S(1)}, bf16[48,512]{1,0:T(8,128)(2,1)S(1)}, bf16[48,512]{1,0:T(8,128)(2,1)S(1)...) custom-call(s32[1,4,8]{2,1,0:T(4,128)S(1)} %bitcast.4, s32[1,8]{1,0:T(1,128)S(1)} %bitcast.5, ...), custom_call_target="tpu_custom_call" | custom-call | flops 1073741824 | bytes 5242880 | tf_op jit(solution)/shard_map/couple/pallas_call | solution.py:164
  21.3 0.0 copy-start.6
  21.3 0.0 copy-start.7
  21.3 1.6 %collective-permute-start.9 = (bf16[80,512]{1,0:T(8,128)(2,1)S(1)}, bf16[80,512]{1,0:T(8,128)(2,1)S(1)}, u32[]{:S(2)}, u32[]{:S(2)}) collective-permute-start(bf16[80,512]{1,0:T(8,128)(2,1)S(1)} %get-tuple-element.16), channel_id=1, source_target_pairs={{0,1},{1,0},{2,3},{3,2},{4,5},{5,4},{6,7},{7,6},{8,9},{9,8},{10,11... | collective-permute-start | bytes 245768 | tf_op jit(solution)/shard_map/ppermute | solution.py:195
  22.9 0.6 %warm.1 = f32[8,128]{1,0:T(8,128)} custom-call(), custom_call_target="tpu_custom_call" | custom-call | flops 20000000000 | bytes 4096 | tf_op jit(solution)/shard_map/warm/pallas_call | solution.py:140
  23.5 2.6 %collective-permute-start.7 = (bf16[48,512]{1,0:T(8,128)(2,1)S(1)}, bf16[48,512]{1,0:T(8,128)(2,1)S(1)}, u32[]{:S(2)}, u32[]{:S(2)}) collective-permute-start(bf16[48,512]{1,0:T(8,128)(2,1)S(1)} %get-tuple-element.13), channel_id=1, source_target_pairs={{0,2},{1,3},{2,0},{3,1},{4,6},{5,7},{6,4},{7,5},{8,10},{9,11},{10,... | collective-permute-start | bytes 147464 | tf_op jit(solution)/shard_map/ppermute | solution.py:195
  26.1 0.2 collective-permute-start.8
  26.4 0.7 %collective-permute-start.6 = (bf16[128,512]{1,0:T(8,128)(2,1)S(1)}, bf16[128,512]{1,0:T(8,128)(2,1)S(1)}, u32[]{:S(2)}, u32[]{:S(2)}) collective-permute-start(bf16[128,512]{1,0:T(8,128)(2,1)S(1)} %get-tuple-element.12), channel_id=1, source_target_pairs={{0,1},{1,0},{2,3},{3,2},{4,5},{5,4},{6,7},{7,6},{8,9},{9,8},{10,11... | collective-permute-start | bytes 393224 | tf_op jit(solution)/shard_map/ppermute | solution.py:195
  27.0 0.0 collective-permute-done.9
  27.1 3.6 %collective-permute-start.10 = (bf16[80,512]{1,0:T(8,128)(2,1)S(1)}, bf16[80,512]{1,0:T(8,128)(2,1)S(1)}, u32[]{:S(2)}, u32[]{:S(2)}) collective-permute-start(bf16[80,512]{1,0:T(8,128)(2,1)S(1)} %add_convert_fusion), channel_id=1, source_target_pairs={{0,2},{1,3},{2,0},{3,1},{4,6},{5,7},{6,4},{7,5},{8,10},{9,11},{10,... | collective-permute-start | bytes 245768 | tf_op jit(solution)/shard_map/ppermute | solution.py:195
  30.6 0.0 collective-permute-done.7
  30.6 1.9 %collective-permute-done.8 = bf16[48,512]{1,0:T(8,128)(2,1)S(1)} collective-permute-done((bf16[48,512]{1,0:T(8,128)(2,1)S(1)}, bf16[48,512]{1,0:T(8,128)(2,1)S(1)}, u32[]{:S(2)}, u32[]{:S(2)}) %collective-permute-start.8) | collective-permute-done | bytes 49184 | tf_op jit(solution)/shard_map/ppermute | solution.py:195
  32.6 1.3 %collective-permute-done.10 = bf16[80,512]{1,0:T(8,128)(2,1)S(1)} collective-permute-done((bf16[80,512]{1,0:T(8,128)(2,1)S(1)}, bf16[80,512]{1,0:T(8,128)(2,1)S(1)}, u32[]{:S(2)}, u32[]{:S(2)}) %collective-permute-start.10) | collective-permute-done | bytes 81952 | tf_op jit(solution)/shard_map/ppermute | solution.py:195
  33.9 0.4 %collective-permute-done.6 = bf16[128,512]{1,0:T(8,128)(2,1)S(1)} collective-permute-done((bf16[128,512]{1,0:T(8,128)(2,1)S(1)}, bf16[128,512]{1,0:T(8,128)(2,1)S(1)}, u32[]{:S(2)}, u32[]{:S(2)}) %collective-permute-start.6) | collective-permute-done | bytes 131104 | tf_op jit(solution)/shard_map/ppermute | solution.py:195
  34.3 0.0 copy-done.6
  34.3 0.0 copy-done.7
  34.3 0.8 %fusion.1 = f32[128,512]{1,0:T(8,128)} fusion(f32[80,512]{1,0:T(8,128)S(1)} %convert_element_type.34, f32[48,512]{1,0:T(8,128)S(1)} %convert_add_fusion, bf16[128,512]{1,0:T(8,128)(2,1)S(1)} %copy-done.2, bf16[128,512]{1,0:T(8,128)(2,1)S(1)} %collective-permute-done.6, bf16[128,512]{1,0:T(8,128)(2,1)S(1)} %get-tuple-element.11, f32[512]{0:T(512)S(1)} %copy-done.6, ...), kind=kLoop, calls=%fused_computation.2 | loop fusion | flops 589824 | bytes 920064 | tf_op jit(solution)/shard_map/add | solution.py:204
  (4 shorter events, 0.1 us)
Async XLA Ops:
  0.0 5.1 %collective-permute-start.3 = (bf16[128,512]{1,0:T(8,128)(2,1)}, bf16[128,512]{1,0:T(8,128)(2,1)S(1)}, u32[]{:S(2)}, u32[]{:S(2)}) collective-permute-start(bf16[128,512]{1,0:T(8,128)(2,1)} %refs_3_.1), channel_id=1, source_target_pairs={{4,0},{0,4},{16,8},{20,12},{8,16},{12,20},{28,24},{24,28},{5,1},{1... | collective-permute-start | bytes 393224 | tf_op jit(solution)/shard_map/ppermute | solution.py:28
  0.5 10.2 %collective-permute-start.1 = (bf16[128,512]{1,0:T(8,128)(2,1)}, bf16[128,512]{1,0:T(8,128)(2,1)S(1)}, u32[]{:S(2)}, u32[]{:S(2)}) collective-permute-start(bf16[128,512]{1,0:T(8,128)(2,1)} %refs_3_.1), channel_id=1, source_target_pairs={{8,0},{12,4},{0,8},{4,12},{20,16},{16,20},{28,24},{24,28},{9,1},{1... | collective-permute-start | bytes 393224 | tf_op jit(solution)/shard_map/ppermute | solution.py:27
  4.5 6.2 %collective-permute-start = (bf16[128,512]{1,0:T(8,128)(2,1)}, bf16[128,512]{1,0:T(8,128)(2,1)S(1)}, u32[]{:S(2)}, u32[]{:S(2)}) collective-permute-start(bf16[128,512]{1,0:T(8,128)(2,1)} %refs_3_.1), channel_id=1, source_target_pairs={{4,0},{0,4},{12,8},{8,12},{24,16},{28,20},{16,24},{20,28},{5,1},{1... | collective-permute-start | bytes 393224 | tf_op jit(solution)/shard_map/ppermute | solution.py:29
  4.5 6.3 %collective-permute-start.2 = (bf16[128,512]{1,0:T(8,128)(2,1)}, bf16[128,512]{1,0:T(8,128)(2,1)S(1)}, u32[]{:S(2)}, u32[]{:S(2)}) collective-permute-start(bf16[128,512]{1,0:T(8,128)(2,1)} %refs_3_.1), channel_id=1, source_target_pairs={{16,4},{24,12},{4,16},{12,24},{17,5},{25,13},{5,17},{13,25},{18,6}... | collective-permute-start | bytes 393224 | tf_op jit(solution)/shard_map/ppermute | solution.py:30
  5.1 5.7 %collective-permute-start.5 = (bf16[128,512]{1,0:T(8,128)(2,1)S(1)}, bf16[128,512]{1,0:T(8,128)(2,1)S(1)}, u32[]{:S(2)}, u32[]{:S(2)}) collective-permute-start(bf16[128,512]{1,0:T(8,128)(2,1)S(1)} %collective-permute-done.3.refs_7_), channel_id=1, source_target_pairs={{0,4},{4,0},{8,12},{12,8},{16,20},{20,16},{24,28},{28,24},{1,5},{5... | collective-permute-start | bytes 393224 | tf_op jit(solution)/shard_map/ppermute | solution.py:43
  10.7 1.4 %collective-permute-start.4 = (bf16[128,512]{1,0:T(8,128)(2,1)S(1)}, bf16[128,512]{1,0:T(8,128)(2,1)S(1)}, u32[]{:S(2)}, u32[]{:S(2)}) collective-permute-start(bf16[128,512]{1,0:T(8,128)(2,1)S(1)} %pick.1), channel_id=1, source_target_pairs={{0,4},{4,0},{8,12},{12,8},{16,20},{20,16},{24,28},{28,24},{1,5},{5... | collective-permute-start | bytes 393224 | tf_op jit(solution)/shard_map/ppermute | solution.py:42
  12.1 2.2 %copy-start = (bf16[8,4,4,128,128]{4,3,2,1,0:T(8,128)(2,1)S(1)}, bf16[8,4,4,128,128]{4,3,2,1,0:T(8,128)(2,1)}, u32[]{:S(2)}) copy-start(bf16[8,4,4,128,128]{4,3,2,1,0:T(8,128)(2,1)} %refs_11_.1) | copy-start | bytes 12582916
  14.3 1.2 %copy-start.1 = (bf16[8,1,4,128,128]{4,3,2,1,0:T(8,128)(2,1)S(1)}, bf16[8,1,4,128,128]{4,3,2,1,0:T(8,128)(2,1)}, u32[]{:S(2)}) copy-start(bf16[8,1,4,128,128]{4,3,2,1,0:T(8,128)(2,1)} %refs_10_.1) | copy-start | bytes 3145732
  15.5 0.9 %copy-start.2 = (bf16[128,512]{1,0:T(8,128)(2,1)S(1)}, bf16[128,512]{1,0:T(8,128)(2,1)}, u32[]{:S(2)}) copy-start(bf16[128,512]{1,0:T(8,128)(2,1)} %refs_3_.1) | copy-start | bytes 393220
  16.4 0.7 %copy-start.3 = (s32[8,4,4]{0,2,1:T(4,128)S(1)}, s32[8,4,4]{0,2,1:T(4,128)}, u32[]{:S(2)}) copy-start(s32[8,4,4]{0,2,1:T(4,128)} %param.13) | copy-start | bytes 1540
  17.1 0.7 %copy-start.4 = (s32[8,1,4]{0,2,1:T(4,128)S(1)}, s32[8,1,4]{0,2,1:T(4,128)}, u32[]{:S(2)}) copy-start(s32[8,1,4]{0,2,1:T(4,128)} %param.10) | copy-start | bytes 388
  17.8 0.7 %copy-start.5 = (s32[8,1]{0,1:T(1,128)S(1)}, s32[8,1]{0,1:T(1,128)}, u32[]{:S(2)}) copy-start(s32[8,1]{0,1:T(1,128)} %param.11) | copy-start | bytes 100
  21.3 13.0 %copy-start.6 = (f32[512]{0:T(512)S(1)}, f32[512]{0:T(512)}, u32[]{:S(2)}) copy-start(f32[512]{0:T(512)} %param.15) | copy-start | bytes 6148
  21.3 13.0 %copy-start.7 = (f32[128]{0:T(128)S(1)}, f32[128]{0:T(128)}, u32[]{:S(2)}) copy-start(f32[128]{0:T(128)} %param.14) | copy-start | bytes 1540
  21.3 5.7 %collective-permute-start.9 = (bf16[80,512]{1,0:T(8,128)(2,1)S(1)}, bf16[80,512]{1,0:T(8,128)(2,1)S(1)}, u32[]{:S(2)}, u32[]{:S(2)}) collective-permute-start(bf16[80,512]{1,0:T(8,128)(2,1)S(1)} %get-tuple-element.16), channel_id=1, source_target_pairs={{0,1},{1,0},{2,3},{3,2},{4,5},{5,4},{6,7},{7,6},{8,9},{9,8},{10,11... | collective-permute-start | bytes 245768 | tf_op jit(solution)/shard_map/ppermute | solution.py:195
  23.5 7.1 %collective-permute-start.7 = (bf16[48,512]{1,0:T(8,128)(2,1)S(1)}, bf16[48,512]{1,0:T(8,128)(2,1)S(1)}, u32[]{:S(2)}, u32[]{:S(2)}) collective-permute-start(bf16[48,512]{1,0:T(8,128)(2,1)S(1)} %get-tuple-element.13), channel_id=1, source_target_pairs={{0,2},{1,3},{2,0},{3,1},{4,6},{5,7},{6,4},{7,5},{8,10},{9,11},{10,... | collective-permute-start | bytes 147464 | tf_op jit(solution)/shard_map/ppermute | solution.py:195
  26.1 6.4 %collective-permute-start.8 = (bf16[48,512]{1,0:T(8,128)(2,1)S(1)}, bf16[48,512]{1,0:T(8,128)(2,1)S(1)}, u32[]{:S(2)}, u32[]{:S(2)}) collective-permute-start(bf16[48,512]{1,0:T(8,128)(2,1)S(1)} %get-tuple-element.14), channel_id=1, source_target_pairs={{0,3},{1,2},{2,1},{3,0},{4,7},{5,6},{6,5},{7,4},{8,11},{9,10},{10,... | collective-permute-start | bytes 147464 | tf_op jit(solution)/shard_map/ppermute | solution.py:195
  26.4 7.9 %collective-permute-start.6 = (bf16[128,512]{1,0:T(8,128)(2,1)S(1)}, bf16[128,512]{1,0:T(8,128)(2,1)S(1)}, u32[]{:S(2)}, u32[]{:S(2)}) collective-permute-start(bf16[128,512]{1,0:T(8,128)(2,1)S(1)} %get-tuple-element.12), channel_id=1, source_target_pairs={{0,1},{1,0},{2,3},{3,2},{4,5},{5,4},{6,7},{7,6},{8,9},{9,8},{10,11... | collective-permute-start | bytes 393224 | tf_op jit(solution)/shard_map/ppermute | solution.py:195
  27.1 6.8 %collective-permute-start.10 = (bf16[80,512]{1,0:T(8,128)(2,1)S(1)}, bf16[80,512]{1,0:T(8,128)(2,1)S(1)}, u32[]{:S(2)}, u32[]{:S(2)}) collective-permute-start(bf16[80,512]{1,0:T(8,128)(2,1)S(1)} %add_convert_fusion), channel_id=1, source_target_pairs={{0,2},{1,3},{2,0},{3,1},{4,6},{5,7},{6,4},{7,5},{8,10},{9,11},{10,... | collective-permute-start | bytes 245768 | tf_op jit(solution)/shard_map/ppermute | solution.py:195

commit v3 on v2

--- a/solution.py
+++ b/solution.py
@@ -67,24 +67,14 @@
 
 
 def couple_kernel(
-    sizes, place_of, tables_from, held, alpha_tiles, beta_tiles, outs, window, coupled, total, tables, semaphores
+    sizes, place_of, tables_from, held, alpha_tiles, beta_tiles, outs, window, coupled, total
 ):
     factors, alpha_slots, local_blocks, beta_slots, groups, by_xor, parts = sizes
     tile_size = total.shape[1]
     own_block, own_group = lax.axis_index("alpha"), lax.axis_index("beta")
-    copies = [
-        pltpu.make_async_copy(source, table, semaphores.at[i])
-        for i, (source, table) in enumerate(zip(tables_from, tables))
-    ]
-    for copy in copies:
-        copy.start()
-    sources, counts, targets = tables
+    sources, counts, targets = (table[...] for table in tables_from)
     for place, piece in held.items():
         window[place] = piece[...]
-    for block in range(total.shape[0]):
-        total[block] = jnp.zeros(total.shape[1:], jnp.float32)
-    for copy in copies:
-        copy.wait()
 
     def alpha(factor):
         places = [place_of(sources[0, slot, factor], own_block) for slot in range(alpha_slots)]
@@ -106,12 +96,12 @@
                 place = away * local_blocks + lax.rem(target, local_blocks)
                 total[place] += added[:, slot * tile_size : (slot + 1) * tile_size]
 
-    def both(factor, _):
+    alpha(0)
+    for block in range(total.shape[0]):
+        total[block] = jnp.zeros(total.shape[1:], jnp.float32)
+    for factor in range(1, factors):
         alpha(factor)
         beta(factor - 1)
-
-    alpha(0)
-    lax.fori_loop(1, factors, both, None, unroll=True)
     beta(factors - 1)
     for (away, first, last), out in zip(parts, outs):
         for block in range(local_blocks):
@@ -156,22 +146,19 @@
         t, n = len(tables), len(held)
         pieces = dict(zip(held, refs[t : t + n]))
         a_ref, b_ref, *outs = refs[t + n : t + n + 2 + len(parts)]
-        window, coupled, total, *near, semaphores = refs[t + n + 2 + len(parts) :]
         couple_kernel(
-            sizes, place_of, refs[:t], pieces, a_ref, b_ref, outs, window, coupled, total, near, semaphores
+            sizes, place_of, refs[:t], pieces, a_ref, b_ref, outs, *refs[t + n + 2 + len(parts) :]
         )
 
     own, *far = pl.pallas_call(
         body,
         out_shape=[jax.ShapeDtypeStruct((last - first, columns), jnp.bfloat16) for _, first, last in parts],
-        in_specs=[pl.BlockSpec(memory_space=pl.ANY)] * len(tables) + [vmem] * (len(held) + 2),
+        in_specs=[vmem] * len(tables) + [vmem] * (len(held) + 2),
         out_specs=[vmem] * len(parts),
         scratch_shapes=[
             pltpu.VMEM((max(held) + 1, tile_size, columns), jnp.bfloat16),
             pltpu.VMEM((factors, tile_size, columns), jnp.bfloat16),
             pltpu.VMEM((groups * local_blocks, tile_size, tile_size), jnp.float32),
-            *[pltpu.SMEM(table.shape, jnp.int32) for table in tables],
-            pltpu.SemaphoreType.DMA((len(tables),)),
         ],
         compiler_params=pltpu.CompilerParams(vmem_limit_bytes=20 * 2**20),
         cost_estimate=pl.CostEstimate(

time: 35.4 us -> 35.1 us (level)
  no operation moved by 1% of the time
where the time goes in v3:
time: 35.1 us; the launch traced here: 34.8 us
  starting transfers between devices  15.8 us (45%)
  waiting for transfers between devices  8.54 us (24%)
  local copies, waits for them, and re-layouts  6.36 us (18%)
  Pallas kernels  3.12 us (9%)
  other arithmetic  0.85 us (2%)
    ppermute x5, starting transfers between devices, send(): return lax.ppermute(value, 'beta', pairs)  8.68 us
    unnamed x16, local copies, waits for them, and re-layouts  6.36 us
    ppermute x1, starting transfers between devices, cube_window(): lax.ppermute(ci_vector, 'alpha', [(i ^ (2 if i in lower else 1), i) for i...  3.97 us
    ppermute x5, waiting for transfers between devices, send(): return lax.ppermute(value, 'beta', pairs)  3.63 us
    ppermute x1, waiting for transfers between devices, cube_window(): lax.ppermute(ci_vector, 'alpha', [(i ^ (2 if i in lower else 1), i) for i...  3.59 us
    pallas_call x1, Pallas kernels, shards(): pl.pallas_call(body, out_shape=[jax.ShapeDtypeStruct((last - first, colum...  2.51 us
    ppermute x1, starting transfers between devices, cube_window(): held[7] = lax.ppermute(cross, 'alpha', swap)  1.96 us
    ppermute x1, waiting for transfers between devices, cube_window(): held[3] = lax.ppermute(beside, 'alpha', swap)  1.31 us
  transfers between devices with their start and end apart: 11, of which 5 were waited for; matrix products, arithmetic and copies ran while one was open for 0% of the time, Pallas kernels for 2%

profile of v3, /device:TPU:0, one launch (start us, length us, event | category | flops | bytes accessed | tf_op | source)
XLA Modules:
  0.0 34.8 jit_solution(10689333939329865356)
XLA Ops:
  0.0 0.5 %collective-permute-start.3 = (bf16[128,512]{1,0:T(8,128)(2,1)}, bf16[128,512]{1,0:T(8,128)(2,1)S(1)}, u32[]{:S(2)}, u32[]{:S(2)}) collective-permute-start(bf16[128,512]{1,0:T(8,128)(2,1)} %refs_3_.1), channel_id=1, source_target_pairs={{4,0},{0,4},{16,8},{20,12},{8,16},{12,20},{28,24},{24,28},{5,1},{1... | collective-permute-start | bytes 393224 | tf_op jit(solution)/shard_map/ppermute | solution.py:28
  0.5 4.0 %collective-permute-start.1 = (bf16[128,512]{1,0:T(8,128)(2,1)}, bf16[128,512]{1,0:T(8,128)(2,1)S(1)}, u32[]{:S(2)}, u32[]{:S(2)}) collective-permute-start(bf16[128,512]{1,0:T(8,128)(2,1)} %refs_3_.1), channel_id=1, source_target_pairs={{8,0},{12,4},{0,8},{4,12},{20,16},{16,20},{28,24},{24,28},{9,1},{1... | collective-permute-start | bytes 393224 | tf_op jit(solution)/shard_map/ppermute | solution.py:27
  4.5 0.0 collective-permute-start
  4.5 0.7 %collective-permute-start.2 = (bf16[128,512]{1,0:T(8,128)(2,1)}, bf16[128,512]{1,0:T(8,128)(2,1)S(1)}, u32[]{:S(2)}, u32[]{:S(2)}) collective-permute-start(bf16[128,512]{1,0:T(8,128)(2,1)} %refs_3_.1), channel_id=1, source_target_pairs={{16,4},{24,12},{4,16},{12,24},{17,5},{25,13},{5,17},{13,25},{18,6}... | collective-permute-start | bytes 393224 | tf_op jit(solution)/shard_map/ppermute | solution.py:30
  5.1 0.0 collective-permute-done.3.refs_7_
  5.1 2.0 %collective-permute-start.5 = (bf16[128,512]{1,0:T(8,128)(2,1)S(1)}, bf16[128,512]{1,0:T(8,128)(2,1)S(1)}, u32[]{:S(2)}, u32[]{:S(2)}) collective-permute-start(bf16[128,512]{1,0:T(8,128)(2,1)S(1)} %collective-permute-done.3.refs_7_), channel_id=1, source_target_pairs={{0,4},{4,0},{8,12},{12,8},{16,20},{20,16},{24,28},{28,24},{1,5},{5... | collective-permute-start | bytes 393224 | tf_op jit(solution)/shard_map/ppermute | solution.py:43
  7.1 3.6 %collective-permute-done.1.first.refs_5_ = bf16[128,512]{1,0:T(8,128)(2,1)S(1)} collective-permute-done((bf16[128,512]{1,0:T(8,128)(2,1)}, bf16[128,512]{1,0:T(8,128)(2,1)S(1)}, u32[]{:S(2)}, u32[]{:S(2)}) %collective-permute-start.1) | collective-permute-done | bytes 131104 | tf_op jit(solution)/shard_map/ppermute | solution.py:27
  10.7 0.0 collective-permute-done.last.refs_4_
  10.7 0.1 collective-permute-start.4
  10.8 0.0 collective-permute-done.2.refs_6_
  10.8 0.0 collective-permute-done.5.refs_9_
  10.8 1.3 %collective-permute-done.4.refs_8_ = bf16[128,512]{1,0:T(8,128)(2,1)S(1)} collective-permute-done((bf16[128,512]{1,0:T(8,128)(2,1)S(1)}, bf16[128,512]{1,0:T(8,128)(2,1)S(1)}, u32[]{:S(2)}, u32[]{:S(2)}) %collective-permute-start.4) | collective-permute-done | bytes 131104 | tf_op jit(solution)/shard_map/ppermute | solution.py:42
  12.1 0.0 copy-start
  12.1 2.2 %copy-done = bf16[8,4,4,128,128]{4,3,2,1,0:T(8,128)(2,1)S(1)} copy-done((bf16[8,4,4,128,128]{4,3,2,1,0:T(8,128)(2,1)S(1)}, bf16[8,4,4,128,128]{4,3,2,1,0:T(8,128)(2,1)}, u32[]{:S(2)}) %copy-start) | copy-done | bytes 4194328
  14.3 0.0 copy-start.1
  14.3 1.2 %copy-done.1 = bf16[8,1,4,128,128]{4,3,2,1,0:T(8,128)(2,1)S(1)} copy-done((bf16[8,1,4,128,128]{4,3,2,1,0:T(8,128)(2,1)S(1)}, bf16[8,1,4,128,128]{4,3,2,1,0:T(8,128)(2,1)}, u32[]{:S(2)}) %copy-start.1) | copy-done | bytes 1048600
  15.5 0.0 copy-start.2
  15.5 0.9 %copy-done.2 = bf16[128,512]{1,0:T(8,128)(2,1)S(1)} copy-done((bf16[128,512]{1,0:T(8,128)(2,1)S(1)}, bf16[128,512]{1,0:T(8,128)(2,1)}, u32[]{:S(2)}) %copy-start.2) | copy-done | bytes 131096
  16.4 0.0 copy-start.3
  16.4 0.7 %copy-done.3 = s32[8,4,4]{0,2,1:T(4,128)S(1)} copy-done((s32[8,4,4]{0,2,1:T(4,128)S(1)}, s32[8,4,4]{0,2,1:T(4,128)}, u32[]{:S(2)}) %copy-start.3) | copy-done | bytes 536
  17.1 0.0 copy-start.4
  17.1 0.7 %copy-done.4 = s32[8,1,4]{0,2,1:T(4,128)S(1)} copy-done((s32[8,1,4]{0,2,1:T(4,128)S(1)}, s32[8,1,4]{0,2,1:T(4,128)}, u32[]{:S(2)}) %copy-start.4) | copy-done | bytes 152
  17.8 0.0 copy-start.5
  17.8 0.7 %copy-done.5 = s32[8,1]{0,1:T(1,128)S(1)} copy-done((s32[8,1]{0,1:T(1,128)S(1)}, s32[8,1]{0,1:T(1,128)}, u32[]{:S(2)}) %copy-start.5) | copy-done | bytes 56
  18.5 2.5 %couple.1 = (bf16[128,512]{1,0:T(8,128)(2,1)S(1)}, bf16[128,512]{1,0:T(8,128)(2,1)S(1)}, bf16[48,512]{1,0:T(8,128)(2,1)S(1)}, bf16[48,512]{1,0:T(8,128)(2,1)S(1)...) custom-call(s32[1,4,8]{2,1,0:T(4,128)S(1)} %bitcast.4, s32[1,8]{1,0:T(1,128)S(1)} %bitcast.5, ...), custom_call_target="tpu_custom_call" | custom-call | flops 1073741824 | bytes 5242880 | tf_op jit(solution)/shard_map/couple/pallas_call | solution.py:153
  21.0 0.0 copy-start.6
  21.0 0.0 copy-start.7
  21.0 1.6 %collective-permute-start.9 = (bf16[80,512]{1,0:T(8,128)(2,1)S(1)}, bf16[80,512]{1,0:T(8,128)(2,1)S(1)}, u32[]{:S(2)}, u32[]{:S(2)}) collective-permute-start(bf16[80,512]{1,0:T(8,128)(2,1)S(1)} %get-tuple-element.16), channel_id=1, source_target_pairs={{0,1},{1,0},{2,3},{3,2},{4,5},{5,4},{6,7},{7,6},{8,9},{9,8},{10,11... | collective-permute-start | bytes 245768 | tf_op jit(solution)/shard_map/ppermute | solution.py:182
  22.7 0.6 %warm.1 = f32[8,128]{1,0:T(8,128)} custom-call(), custom_call_target="tpu_custom_call" | custom-call | flops 20000000000 | bytes 4096 | tf_op jit(solution)/shard_map/warm/pallas_call | solution.py:130
  23.3 2.6 %collective-permute-start.7 = (bf16[48,512]{1,0:T(8,128)(2,1)S(1)}, bf16[48,512]{1,0:T(8,128)(2,1)S(1)}, u32[]{:S(2)}, u32[]{:S(2)}) collective-permute-start(bf16[48,512]{1,0:T(8,128)(2,1)S(1)} %get-tuple-element.13), channel_id=1, source_target_pairs={{0,2},{1,3},{2,0},{3,1},{4,6},{5,7},{6,4},{7,5},{8,10},{9,11},{10,... | collective-permute-start | bytes 147464 | tf_op jit(solution)/shard_map/ppermute | solution.py:182
  25.8 0.2 collective-permute-start.8
  26.1 0.7 %collective-permute-start.6 = (bf16[128,512]{1,0:T(8,128)(2,1)S(1)}, bf16[128,512]{1,0:T(8,128)(2,1)S(1)}, u32[]{:S(2)}, u32[]{:S(2)}) collective-permute-start(bf16[128,512]{1,0:T(8,128)(2,1)S(1)} %get-tuple-element.12), channel_id=1, source_target_pairs={{0,1},{1,0},{2,3},{3,2},{4,5},{5,4},{6,7},{7,6},{8,9},{9,8},{10,11... | collective-permute-start | bytes 393224 | tf_op jit(solution)/shard_map/ppermute | solution.py:182
  26.8 0.0 collective-permute-done.9
  26.8 3.5 %collective-permute-start.10 = (bf16[80,512]{1,0:T(8,128)(2,1)S(1)}, bf16[80,512]{1,0:T(8,128)(2,1)S(1)}, u32[]{:S(2)}, u32[]{:S(2)}) collective-permute-start(bf16[80,512]{1,0:T(8,128)(2,1)S(1)} %add_convert_fusion), channel_id=1, source_target_pairs={{0,2},{1,3},{2,0},{3,1},{4,6},{5,7},{6,4},{7,5},{8,10},{9,11},{10,... | collective-permute-start | bytes 245768 | tf_op jit(solution)/shard_map/ppermute | solution.py:182
  30.3 0.0 collective-permute-done.7
  30.3 1.9 %collective-permute-done.8 = bf16[48,512]{1,0:T(8,128)(2,1)S(1)} collective-permute-done((bf16[48,512]{1,0:T(8,128)(2,1)S(1)}, bf16[48,512]{1,0:T(8,128)(2,1)S(1)}, u32[]{:S(2)}, u32[]{:S(2)}) %collective-permute-start.8) | collective-permute-done | bytes 49184 | tf_op jit(solution)/shard_map/ppermute | solution.py:182
  32.3 1.3 %collective-permute-done.10 = bf16[80,512]{1,0:T(8,128)(2,1)S(1)} collective-permute-done((bf16[80,512]{1,0:T(8,128)(2,1)S(1)}, bf16[80,512]{1,0:T(8,128)(2,1)S(1)}, u32[]{:S(2)}, u32[]{:S(2)}) %collective-permute-start.10) | collective-permute-done | bytes 81952 | tf_op jit(solution)/shard_map/ppermute | solution.py:182
  33.6 0.4 %collective-permute-done.6 = bf16[128,512]{1,0:T(8,128)(2,1)S(1)} collective-permute-done((bf16[128,512]{1,0:T(8,128)(2,1)S(1)}, bf16[128,512]{1,0:T(8,128)(2,1)S(1)}, u32[]{:S(2)}, u32[]{:S(2)}) %collective-permute-start.6) | collective-permute-done | bytes 131104 | tf_op jit(solution)/shard_map/ppermute | solution.py:182
  34.0 0.0 copy-done.6
  34.0 0.0 copy-done.7
  34.0 0.8 %fusion.1 = f32[128,512]{1,0:T(8,128)} fusion(f32[80,512]{1,0:T(8,128)S(1)} %convert_element_type.34, f32[48,512]{1,0:T(8,128)S(1)} %convert_add_fusion, bf16[128,512]{1,0:T(8,128)(2,1)S(1)} %copy-done.2, bf16[128,512]{1,0:T(8,128)(2,1)S(1)} %collective-permute-done.6, bf16[128,512]{1,0:T(8,128)(2,1)S(1)} %get-tuple-element.11, f32[512]{0:T(512)S(1)} %copy-done.6, ...), kind=kLoop, calls=%fused_computation.2 | loop fusion | flops 589824 | bytes 920064 | tf_op jit(solution)/shard_map/add | solution.py:191
  (4 shorter events, 0.1 us)
Async XLA Ops:
  0.0 5.1 %collective-permute-start.3 = (bf16[128,512]{1,0:T(8,128)(2,1)}, bf16[128,512]{1,0:T(8,128)(2,1)S(1)}, u32[]{:S(2)}, u32[]{:S(2)}) collective-permute-start(bf16[128,512]{1,0:T(8,128)(2,1)} %refs_3_.1), channel_id=1, source_target_pairs={{4,0},{0,4},{16,8},{20,12},{8,16},{12,20},{28,24},{24,28},{5,1},{1... | collective-permute-start | bytes 393224 | tf_op jit(solution)/shard_map/ppermute | solution.py:28
  0.5 10.2 %collective-permute-start.1 = (bf16[128,512]{1,0:T(8,128)(2,1)}, bf16[128,512]{1,0:T(8,128)(2,1)S(1)}, u32[]{:S(2)}, u32[]{:S(2)}) collective-permute-start(bf16[128,512]{1,0:T(8,128)(2,1)} %refs_3_.1), channel_id=1, source_target_pairs={{8,0},{12,4},{0,8},{4,12},{20,16},{16,20},{28,24},{24,28},{9,1},{1... | collective-permute-start | bytes 393224 | tf_op jit(solution)/shard_map/ppermute | solution.py:27
  4.5 6.2 %collective-permute-start = (bf16[128,512]{1,0:T(8,128)(2,1)}, bf16[128,512]{1,0:T(8,128)(2,1)S(1)}, u32[]{:S(2)}, u32[]{:S(2)}) collective-permute-start(bf16[128,512]{1,0:T(8,128)(2,1)} %refs_3_.1), channel_id=1, source_target_pairs={{4,0},{0,4},{12,8},{8,12},{24,16},{28,20},{16,24},{20,28},{5,1},{1... | collective-permute-start | bytes 393224 | tf_op jit(solution)/shard_map/ppermute | solution.py:29
  4.5 6.3 %collective-permute-start.2 = (bf16[128,512]{1,0:T(8,128)(2,1)}, bf16[128,512]{1,0:T(8,128)(2,1)S(1)}, u32[]{:S(2)}, u32[]{:S(2)}) collective-permute-start(bf16[128,512]{1,0:T(8,128)(2,1)} %refs_3_.1), channel_id=1, source_target_pairs={{16,4},{24,12},{4,16},{12,24},{17,5},{25,13},{5,17},{13,25},{18,6}... | collective-permute-start | bytes 393224 | tf_op jit(solution)/shard_map/ppermute | solution.py:30
  5.1 5.7 %collective-permute-start.5 = (bf16[128,512]{1,0:T(8,128)(2,1)S(1)}, bf16[128,512]{1,0:T(8,128)(2,1)S(1)}, u32[]{:S(2)}, u32[]{:S(2)}) collective-permute-start(bf16[128,512]{1,0:T(8,128)(2,1)S(1)} %collective-permute-done.3.refs_7_), channel_id=1, source_target_pairs={{0,4},{4,0},{8,12},{12,8},{16,20},{20,16},{24,28},{28,24},{1,5},{5... | collective-permute-start | bytes 393224 | tf_op jit(solution)/shard_map/ppermute | solution.py:43
  10.7 1.4 %collective-permute-start.4 = (bf16[128,512]{1,0:T(8,128)(2,1)S(1)}, bf16[128,512]{1,0:T(8,128)(2,1)S(1)}, u32[]{:S(2)}, u32[]{:S(2)}) collective-permute-start(bf16[128,512]{1,0:T(8,128)(2,1)S(1)} %pick.1), channel_id=1, source_target_pairs={{0,4},{4,0},{8,12},{12,8},{16,20},{20,16},{24,28},{28,24},{1,5},{5... | collective-permute-start | bytes 393224 | tf_op jit(solution)/shard_map/ppermute | solution.py:42
  12.1 2.2 %copy-start = (bf16[8,4,4,128,128]{4,3,2,1,0:T(8,128)(2,1)S(1)}, bf16[8,4,4,128,128]{4,3,2,1,0:T(8,128)(2,1)}, u32[]{:S(2)}) copy-start(bf16[8,4,4,128,128]{4,3,2,1,0:T(8,128)(2,1)} %refs_11_.1) | copy-start | bytes 12582916
  14.3 1.2 %copy-start.1 = (bf16[8,1,4,128,128]{4,3,2,1,0:T(8,128)(2,1)S(1)}, bf16[8,1,4,128,128]{4,3,2,1,0:T(8,128)(2,1)}, u32[]{:S(2)}) copy-start(bf16[8,1,4,128,128]{4,3,2,1,0:T(8,128)(2,1)} %refs_10_.1) | copy-start | bytes 3145732
  15.5 0.9 %copy-start.2 = (bf16[128,512]{1,0:T(8,128)(2,1)S(1)}, bf16[128,512]{1,0:T(8,128)(2,1)}, u32[]{:S(2)}) copy-start(bf16[128,512]{1,0:T(8,128)(2,1)} %refs_3_.1) | copy-start | bytes 393220
  16.4 0.7 %copy-start.3 = (s32[8,4,4]{0,2,1:T(4,128)S(1)}, s32[8,4,4]{0,2,1:T(4,128)}, u32[]{:S(2)}) copy-start(s32[8,4,4]{0,2,1:T(4,128)} %param.13) | copy-start | bytes 1540
  17.1 0.7 %copy-start.4 = (s32[8,1,4]{0,2,1:T(4,128)S(1)}, s32[8,1,4]{0,2,1:T(4,128)}, u32[]{:S(2)}) copy-start(s32[8,1,4]{0,2,1:T(4,128)} %param.10) | copy-start | bytes 388
  17.8 0.7 %copy-start.5 = (s32[8,1]{0,1:T(1,128)S(1)}, s32[8,1]{0,1:T(1,128)}, u32[]{:S(2)}) copy-start(s32[8,1]{0,1:T(1,128)} %param.11) | copy-start | bytes 100
  21.0 13.0 %copy-start.6 = (f32[512]{0:T(512)S(1)}, f32[512]{0:T(512)}, u32[]{:S(2)}) copy-start(f32[512]{0:T(512)} %param.15) | copy-start | bytes 6148
  21.0 13.0 %copy-start.7 = (f32[128]{0:T(128)S(1)}, f32[128]{0:T(128)}, u32[]{:S(2)}) copy-start(f32[128]{0:T(128)} %param.14) | copy-start | bytes 1540
  21.0 5.7 %collective-permute-start.9 = (bf16[80,512]{1,0:T(8,128)(2,1)S(1)}, bf16[80,512]{1,0:T(8,128)(2,1)S(1)}, u32[]{:S(2)}, u32[]{:S(2)}) collective-permute-start(bf16[80,512]{1,0:T(8,128)(2,1)S(1)} %get-tuple-element.16), channel_id=1, source_target_pairs={{0,1},{1,0},{2,3},{3,2},{4,5},{5,4},{6,7},{7,6},{8,9},{9,8},{10,11... | collective-permute-start | bytes 245768 | tf_op jit(solution)/shard_map/ppermute | solution.py:182
  23.3 7.1 %collective-permute-start.7 = (bf16[48,512]{1,0:T(8,128)(2,1)S(1)}, bf16[48,512]{1,0:T(8,128)(2,1)S(1)}, u32[]{:S(2)}, u32[]{:S(2)}) collective-permute-start(bf16[48,512]{1,0:T(8,128)(2,1)S(1)} %get-tuple-element.13), channel_id=1, source_target_pairs={{0,2},{1,3},{2,0},{3,1},{4,6},{5,7},{6,4},{7,5},{8,10},{9,11},{10,... | collective-permute-start | bytes 147464 | tf_op jit(solution)/shard_map/ppermute | solution.py:182
  25.8 6.4 %collective-permute-start.8 = (bf16[48,512]{1,0:T(8,128)(2,1)S(1)}, bf16[48,512]{1,0:T(8,128)(2,1)S(1)}, u32[]{:S(2)}, u32[]{:S(2)}) collective-permute-start(bf16[48,512]{1,0:T(8,128)(2,1)S(1)} %get-tuple-element.14), channel_id=1, source_target_pairs={{0,3},{1,2},{2,1},{3,0},{4,7},{5,6},{6,5},{7,4},{8,11},{9,10},{10,... | collective-permute-start | bytes 147464 | tf_op jit(solution)/shard_map/ppermute | solution.py:182
  26.1 7.9 %collective-permute-start.6 = (bf16[128,512]{1,0:T(8,128)(2,1)S(1)}, bf16[128,512]{1,0:T(8,128)(2,1)S(1)}, u32[]{:S(2)}, u32[]{:S(2)}) collective-permute-start(bf16[128,512]{1,0:T(8,128)(2,1)S(1)} %get-tuple-element.12), channel_id=1, source_target_pairs={{0,1},{1,0},{2,3},{3,2},{4,5},{5,4},{6,7},{7,6},{8,9},{9,8},{10,11... | collective-permute-start | bytes 393224 | tf_op jit(solution)/shard_map/ppermute | solution.py:182
  26.8 6.8 %collective-permute-start.10 = (bf16[80,512]{1,0:T(8,128)(2,1)S(1)}, bf16[80,512]{1,0:T(8,128)(2,1)S(1)}, u32[]{:S(2)}, u32[]{:S(2)}) collective-permute-start(bf16[80,512]{1,0:T(8,128)(2,1)S(1)} %add_convert_fusion), channel_id=1, source_target_pairs={{0,2},{1,3},{2,0},{3,1},{4,6},{5,7},{6,4},{7,5},{8,10},{9,11},{10,... | collective-permute-start | bytes 245768 | tf_op jit(solution)/shard_map/ppermute | solution.py:182

commit v4 on v3

--- a/solution.py
+++ b/solution.py
@@ -7,6 +7,7 @@
 
 
 BAND = 3
+LAG = 3
 WARM_FLOPS = 2 * 10**10
 
 
@@ -101,8 +102,10 @@
         total[block] = jnp.zeros(total.shape[1:], jnp.float32)
     for factor in range(1, factors):
         alpha(factor)
-        beta(factor - 1)
-    beta(factors - 1)
+        if factor >= LAG:
+            beta(factor - LAG)
+    for factor in range(max(factors - LAG, 0), factors):
+        beta(factor)
     for (away, first, last), out in zip(parts, outs):
         for block in range(local_blocks):
             value = total[away * local_blocks + block, first:last].astype(jnp.bfloat16)

time: 35.1 us -> 34.9 us (level)
  no operation moved by 1% of the time
where the time goes in v4:
time: 34.9 us; the launch traced here: 34.6 us
  starting transfers between devices  15.8 us (45%)
  waiting for transfers between devices  8.54 us (24%)
  local copies, waits for them, and re-layouts  6.36 us (18%)
  Pallas kernels  2.97 us (9%)
  other arithmetic  0.85 us (2%)
    ppermute x5, starting transfers between devices, send(): return lax.ppermute(value, 'beta', pairs)  8.68 us
    unnamed x16, local copies, waits for them, and re-layouts  6.36 us
    ppermute x1, starting transfers between devices, cube_window(): lax.ppermute(ci_vector, 'alpha', [(i ^ (2 if i in lower else 1), i) for i...  3.97 us
    ppermute x5, waiting for transfers between devices, send(): return lax.ppermute(value, 'beta', pairs)  3.62 us
    ppermute x1, waiting for transfers between devices, cube_window(): lax.ppermute(ci_vector, 'alpha', [(i ^ (2 if i in lower else 1), i) for i...  3.59 us
    pallas_call x1, Pallas kernels, shards(): pl.pallas_call(body, out_shape=[jax.ShapeDtypeStruct((last - first, colum...  2.36 us
    ppermute x1, starting transfers between devices, cube_window(): held[7] = lax.ppermute(cross, 'alpha', swap)  1.96 us
    ppermute x1, waiting for transfers between devices, cube_window(): held[3] = lax.ppermute(beside, 'alpha', swap)  1.31 us
  transfers between devices with their start and end apart: 11, of which 5 were waited for; matrix products, arithmetic and copies ran while one was open for 0% of the time, Pallas kernels for 2%

profile of v4, /device:TPU:0, one launch (start us, length us, event | category | flops | bytes accessed | tf_op | source)
XLA Modules:
  0.0 34.6 jit_solution(11637026103916209086)
XLA Ops:
  0.0 0.5 %collective-permute-start.3 = (bf16[128,512]{1,0:T(8,128)(2,1)}, bf16[128,512]{1,0:T(8,128)(2,1)S(1)}, u32[]{:S(2)}, u32[]{:S(2)}) collective-permute-start(bf16[128,512]{1,0:T(8,128)(2,1)} %refs_3_.1), channel_id=1, source_target_pairs={{4,0},{0,4},{16,8},{20,12},{8,16},{12,20},{28,24},{24,28},{5,1},{1... | collective-permute-start | bytes 393224 | tf_op jit(solution)/shard_map/ppermute | solution.py:29
  0.5 4.0 %collective-permute-start.1 = (bf16[128,512]{1,0:T(8,128)(2,1)}, bf16[128,512]{1,0:T(8,128)(2,1)S(1)}, u32[]{:S(2)}, u32[]{:S(2)}) collective-permute-start(bf16[128,512]{1,0:T(8,128)(2,1)} %refs_3_.1), channel_id=1, source_target_pairs={{8,0},{12,4},{0,8},{4,12},{20,16},{16,20},{28,24},{24,28},{9,1},{1... | collective-permute-start | bytes 393224 | tf_op jit(solution)/shard_map/ppermute | solution.py:28
  4.5 0.0 collective-permute-start
  4.5 0.7 %collective-permute-start.2 = (bf16[128,512]{1,0:T(8,128)(2,1)}, bf16[128,512]{1,0:T(8,128)(2,1)S(1)}, u32[]{:S(2)}, u32[]{:S(2)}) collective-permute-start(bf16[128,512]{1,0:T(8,128)(2,1)} %refs_3_.1), channel_id=1, source_target_pairs={{16,4},{24,12},{4,16},{12,24},{17,5},{25,13},{5,17},{13,25},{18,6}... | collective-permute-start | bytes 393224 | tf_op jit(solution)/shard_map/ppermute | solution.py:31
  5.1 0.0 collective-permute-done.3.refs_7_
  5.1 2.0 %collective-permute-start.5 = (bf16[128,512]{1,0:T(8,128)(2,1)S(1)}, bf16[128,512]{1,0:T(8,128)(2,1)S(1)}, u32[]{:S(2)}, u32[]{:S(2)}) collective-permute-start(bf16[128,512]{1,0:T(8,128)(2,1)S(1)} %collective-permute-done.3.refs_7_), channel_id=1, source_target_pairs={{0,4},{4,0},{8,12},{12,8},{16,20},{20,16},{24,28},{28,24},{1,5},{5... | collective-permute-start | bytes 393224 | tf_op jit(solution)/shard_map/ppermute | solution.py:44
  7.1 3.6 %collective-permute-done.1.first.refs_5_ = bf16[128,512]{1,0:T(8,128)(2,1)S(1)} collective-permute-done((bf16[128,512]{1,0:T(8,128)(2,1)}, bf16[128,512]{1,0:T(8,128)(2,1)S(1)}, u32[]{:S(2)}, u32[]{:S(2)}) %collective-permute-start.1) | collective-permute-done | bytes 131104 | tf_op jit(solution)/shard_map/ppermute | solution.py:28
  10.7 0.0 collective-permute-done.last.refs_4_
  10.7 0.1 collective-permute-start.4
  10.8 0.0 collective-permute-done.2.refs_6_
  10.8 0.0 collective-permute-done.5.refs_9_
  10.8 1.3 %collective-permute-done.4.refs_8_ = bf16[128,512]{1,0:T(8,128)(2,1)S(1)} collective-permute-done((bf16[128,512]{1,0:T(8,128)(2,1)S(1)}, bf16[128,512]{1,0:T(8,128)(2,1)S(1)}, u32[]{:S(2)}, u32[]{:S(2)}) %collective-permute-start.4) | collective-permute-done | bytes 131104 | tf_op jit(solution)/shard_map/ppermute | solution.py:43
  12.1 0.0 copy-start
  12.1 2.2 %copy-done = bf16[8,4,4,128,128]{4,3,2,1,0:T(8,128)(2,1)S(1)} copy-done((bf16[8,4,4,128,128]{4,3,2,1,0:T(8,128)(2,1)S(1)}, bf16[8,4,4,128,128]{4,3,2,1,0:T(8,128)(2,1)}, u32[]{:S(2)}) %copy-start) | copy-done | bytes 4194328
  14.3 0.0 copy-start.1
  14.3 1.2 %copy-done.1 = bf16[8,1,4,128,128]{4,3,2,1,0:T(8,128)(2,1)S(1)} copy-done((bf16[8,1,4,128,128]{4,3,2,1,0:T(8,128)(2,1)S(1)}, bf16[8,1,4,128,128]{4,3,2,1,0:T(8,128)(2,1)}, u32[]{:S(2)}) %copy-start.1) | copy-done | bytes 1048600
  15.5 0.0 copy-start.2
  15.5 0.9 %copy-done.2 = bf16[128,512]{1,0:T(8,128)(2,1)S(1)} copy-done((bf16[128,512]{1,0:T(8,128)(2,1)S(1)}, bf16[128,512]{1,0:T(8,128)(2,1)}, u32[]{:S(2)}) %copy-start.2) | copy-done | bytes 131096
  16.4 0.0 copy-start.3
  16.4 0.7 %copy-done.3 = s32[8,4,4]{0,2,1:T(4,128)S(1)} copy-done((s32[8,4,4]{0,2,1:T(4,128)S(1)}, s32[8,4,4]{0,2,1:T(4,128)}, u32[]{:S(2)}) %copy-start.3) | copy-done | bytes 536
  17.1 0.0 copy-start.4
  17.1 0.7 %copy-done.4 = s32[8,1,4]{0,2,1:T(4,128)S(1)} copy-done((s32[8,1,4]{0,2,1:T(4,128)S(1)}, s32[8,1,4]{0,2,1:T(4,128)}, u32[]{:S(2)}) %copy-start.4) | copy-done | bytes 152
  17.8 0.0 copy-start.5
  17.8 0.7 %copy-done.5 = s32[8,1]{0,1:T(1,128)S(1)} copy-done((s32[8,1]{0,1:T(1,128)S(1)}, s32[8,1]{0,1:T(1,128)}, u32[]{:S(2)}) %copy-start.5) | copy-done | bytes 56
  18.5 2.4 %couple.1 = (bf16[128,512]{1,0:T(8,128)(2,1)S(1)}, bf16[128,512]{1,0:T(8,128)(2,1)S(1)}, bf16[48,512]{1,0:T(8,128)(2,1)S(1)}, bf16[48,512]{1,0:T(8,128)(2,1)S(1)...) custom-call(s32[1,4,8]{2,1,0:T(4,128)S(1)} %bitcast.4, s32[1,8]{1,0:T(1,128)S(1)} %bitcast.5, ...), custom_call_target="tpu_custom_call" | custom-call | flops 1073741824 | bytes 5242880 | tf_op jit(solution)/shard_map/couple/pallas_call | solution.py:156
  20.9 0.0 copy-start.6
  20.9 0.0 copy-start.7
  20.9 1.6 %collective-permute-start.9 = (bf16[80,512]{1,0:T(8,128)(2,1)S(1)}, bf16[80,512]{1,0:T(8,128)(2,1)S(1)}, u32[]{:S(2)}, u32[]{:S(2)}) collective-permute-start(bf16[80,512]{1,0:T(8,128)(2,1)S(1)} %get-tuple-element.16), channel_id=1, source_target_pairs={{0,1},{1,0},{2,3},{3,2},{4,5},{5,4},{6,7},{7,6},{8,9},{9,8},{10,11... | collective-permute-start | bytes 245768 | tf_op jit(solution)/shard_map/ppermute | solution.py:185
  22.5 0.6 %warm.1 = f32[8,128]{1,0:T(8,128)} custom-call(), custom_call_target="tpu_custom_call" | custom-call | flops 20000000000 | bytes 4096 | tf_op jit(solution)/shard_map/warm/pallas_call | solution.py:133
  23.1 2.6 %collective-permute-start.7 = (bf16[48,512]{1,0:T(8,128)(2,1)S(1)}, bf16[48,512]{1,0:T(8,128)(2,1)S(1)}, u32[]{:S(2)}, u32[]{:S(2)}) collective-permute-start(bf16[48,512]{1,0:T(8,128)(2,1)S(1)} %get-tuple-element.13), channel_id=1, source_target_pairs={{0,2},{1,3},{2,0},{3,1},{4,6},{5,7},{6,4},{7,5},{8,10},{9,11},{10,... | collective-permute-start | bytes 147464 | tf_op jit(solution)/shard_map/ppermute | solution.py:185
  25.7 0.2 collective-permute-start.8
  25.9 0.7 %collective-permute-start.6 = (bf16[128,512]{1,0:T(8,128)(2,1)S(1)}, bf16[128,512]{1,0:T(8,128)(2,1)S(1)}, u32[]{:S(2)}, u32[]{:S(2)}) collective-permute-start(bf16[128,512]{1,0:T(8,128)(2,1)S(1)} %get-tuple-element.12), channel_id=1, source_target_pairs={{0,1},{1,0},{2,3},{3,2},{4,5},{5,4},{6,7},{7,6},{8,9},{9,8},{10,11... | collective-permute-start | bytes 393224 | tf_op jit(solution)/shard_map/ppermute | solution.py:185
  26.6 0.0 collective-permute-done.9
  26.6 3.6 %collective-permute-start.10 = (bf16[80,512]{1,0:T(8,128)(2,1)S(1)}, bf16[80,512]{1,0:T(8,128)(2,1)S(1)}, u32[]{:S(2)}, u32[]{:S(2)}) collective-permute-start(bf16[80,512]{1,0:T(8,128)(2,1)S(1)} %add_convert_fusion), channel_id=1, source_target_pairs={{0,2},{1,3},{2,0},{3,1},{4,6},{5,7},{6,4},{7,5},{8,10},{9,11},{10,... | collective-permute-start | bytes 245768 | tf_op jit(solution)/shard_map/ppermute | solution.py:185
  30.2 0.0 collective-permute-done.7
  30.2 1.9 %collective-permute-done.8 = bf16[48,512]{1,0:T(8,128)(2,1)S(1)} collective-permute-done((bf16[48,512]{1,0:T(8,128)(2,1)S(1)}, bf16[48,512]{1,0:T(8,128)(2,1)S(1)}, u32[]{:S(2)}, u32[]{:S(2)}) %collective-permute-start.8) | collective-permute-done | bytes 49184 | tf_op jit(solution)/shard_map/ppermute | solution.py:185
  32.1 1.3 %collective-permute-done.10 = bf16[80,512]{1,0:T(8,128)(2,1)S(1)} collective-permute-done((bf16[80,512]{1,0:T(8,128)(2,1)S(1)}, bf16[80,512]{1,0:T(8,128)(2,1)S(1)}, u32[]{:S(2)}, u32[]{:S(2)}) %collective-permute-start.10) | collective-permute-done | bytes 81952 | tf_op jit(solution)/shard_map/ppermute | solution.py:185
  33.4 0.4 %collective-permute-done.6 = bf16[128,512]{1,0:T(8,128)(2,1)S(1)} collective-permute-done((bf16[128,512]{1,0:T(8,128)(2,1)S(1)}, bf16[128,512]{1,0:T(8,128)(2,1)S(1)}, u32[]{:S(2)}, u32[]{:S(2)}) %collective-permute-start.6) | collective-permute-done | bytes 131104 | tf_op jit(solution)/shard_map/ppermute | solution.py:185
  33.8 0.0 copy-done.6
  33.8 0.0 copy-done.7
  33.8 0.8 %fusion.1 = f32[128,512]{1,0:T(8,128)} fusion(f32[80,512]{1,0:T(8,128)S(1)} %convert_element_type.34, f32[48,512]{1,0:T(8,128)S(1)} %convert_add_fusion, bf16[128,512]{1,0:T(8,128)(2,1)S(1)} %copy-done.2, bf16[128,512]{1,0:T(8,128)(2,1)S(1)} %collective-permute-done.6, bf16[128,512]{1,0:T(8,128)(2,1)S(1)} %get-tuple-element.11, f32[512]{0:T(512)S(1)} %copy-done.6, ...), kind=kLoop, calls=%fused_computation.2 | loop fusion | flops 589824 | bytes 920064 | tf_op jit(solution)/shard_map/add | solution.py:194
  (4 shorter events, 0.1 us)
Async XLA Ops:
  0.0 5.1 %collective-permute-start.3 = (bf16[128,512]{1,0:T(8,128)(2,1)}, bf16[128,512]{1,0:T(8,128)(2,1)S(1)}, u32[]{:S(2)}, u32[]{:S(2)}) collective-permute-start(bf16[128,512]{1,0:T(8,128)(2,1)} %refs_3_.1), channel_id=1, source_target_pairs={{4,0},{0,4},{16,8},{20,12},{8,16},{12,20},{28,24},{24,28},{5,1},{1... | collective-permute-start | bytes 393224 | tf_op jit(solution)/shard_map/ppermute | solution.py:29
  0.5 10.2 %collective-permute-start.1 = (bf16[128,512]{1,0:T(8,128)(2,1)}, bf16[128,512]{1,0:T(8,128)(2,1)S(1)}, u32[]{:S(2)}, u32[]{:S(2)}) collective-permute-start(bf16[128,512]{1,0:T(8,128)(2,1)} %refs_3_.1), channel_id=1, source_target_pairs={{8,0},{12,4},{0,8},{4,12},{20,16},{16,20},{28,24},{24,28},{9,1},{1... | collective-permute-start | bytes 393224 | tf_op jit(solution)/shard_map/ppermute | solution.py:28
  4.5 6.2 %collective-permute-start = (bf16[128,512]{1,0:T(8,128)(2,1)}, bf16[128,512]{1,0:T(8,128)(2,1)S(1)}, u32[]{:S(2)}, u32[]{:S(2)}) collective-permute-start(bf16[128,512]{1,0:T(8,128)(2,1)} %refs_3_.1), channel_id=1, source_target_pairs={{4,0},{0,4},{12,8},{8,12},{24,16},{28,20},{16,24},{20,28},{5,1},{1... | collective-permute-start | bytes 393224 | tf_op jit(solution)/shard_map/ppermute | solution.py:30
  4.5 6.3 %collective-permute-start.2 = (bf16[128,512]{1,0:T(8,128)(2,1)}, bf16[128,512]{1,0:T(8,128)(2,1)S(1)}, u32[]{:S(2)}, u32[]{:S(2)}) collective-permute-start(bf16[128,512]{1,0:T(8,128)(2,1)} %refs_3_.1), channel_id=1, source_target_pairs={{16,4},{24,12},{4,16},{12,24},{17,5},{25,13},{5,17},{13,25},{18,6}... | collective-permute-start | bytes 393224 | tf_op jit(solution)/shard_map/ppermute | solution.py:31
  5.1 5.7 %collective-permute-start.5 = (bf16[128,512]{1,0:T(8,128)(2,1)S(1)}, bf16[128,512]{1,0:T(8,128)(2,1)S(1)}, u32[]{:S(2)}, u32[]{:S(2)}) collective-permute-start(bf16[128,512]{1,0:T(8,128)(2,1)S(1)} %collective-permute-done.3.refs_7_), channel_id=1, source_target_pairs={{0,4},{4,0},{8,12},{12,8},{16,20},{20,16},{24,28},{28,24},{1,5},{5... | collective-permute-start | bytes 393224 | tf_op jit(solution)/shard_map/ppermute | solution.py:44
  10.7 1.4 %collective-permute-start.4 = (bf16[128,512]{1,0:T(8,128)(2,1)S(1)}, bf16[128,512]{1,0:T(8,128)(2,1)S(1)}, u32[]{:S(2)}, u32[]{:S(2)}) collective-permute-start(bf16[128,512]{1,0:T(8,128)(2,1)S(1)} %pick.1), channel_id=1, source_target_pairs={{0,4},{4,0},{8,12},{12,8},{16,20},{20,16},{24,28},{28,24},{1,5},{5... | collective-permute-start | bytes 393224 | tf_op jit(solution)/shard_map/ppermute | solution.py:43
  12.1 2.2 %copy-start = (bf16[8,4,4,128,128]{4,3,2,1,0:T(8,128)(2,1)S(1)}, bf16[8,4,4,128,128]{4,3,2,1,0:T(8,128)(2,1)}, u32[]{:S(2)}) copy-start(bf16[8,4,4,128,128]{4,3,2,1,0:T(8,128)(2,1)} %refs_11_.1) | copy-start | bytes 12582916
  14.3 1.2 %copy-start.1 = (bf16[8,1,4,128,128]{4,3,2,1,0:T(8,128)(2,1)S(1)}, bf16[8,1,4,128,128]{4,3,2,1,0:T(8,128)(2,1)}, u32[]{:S(2)}) copy-start(bf16[8,1,4,128,128]{4,3,2,1,0:T(8,128)(2,1)} %refs_10_.1) | copy-start | bytes 3145732
  15.5 0.9 %copy-start.2 = (bf16[128,512]{1,0:T(8,128)(2,1)S(1)}, bf16[128,512]{1,0:T(8,128)(2,1)}, u32[]{:S(2)}) copy-start(bf16[128,512]{1,0:T(8,128)(2,1)} %refs_3_.1) | copy-start | bytes 393220
  16.4 0.7 %copy-start.3 = (s32[8,4,4]{0,2,1:T(4,128)S(1)}, s32[8,4,4]{0,2,1:T(4,128)}, u32[]{:S(2)}) copy-start(s32[8,4,4]{0,2,1:T(4,128)} %param.13) | copy-start | bytes 1540
  17.1 0.7 %copy-start.4 = (s32[8,1,4]{0,2,1:T(4,128)S(1)}, s32[8,1,4]{0,2,1:T(4,128)}, u32[]{:S(2)}) copy-start(s32[8,1,4]{0,2,1:T(4,128)} %param.10) | copy-start | bytes 388
  17.8 0.7 %copy-start.5 = (s32[8,1]{0,1:T(1,128)S(1)}, s32[8,1]{0,1:T(1,128)}, u32[]{:S(2)}) copy-start(s32[8,1]{0,1:T(1,128)} %param.11) | copy-start | bytes 100
  20.9 13.0 %copy-start.6 = (f32[512]{0:T(512)S(1)}, f32[512]{0:T(512)}, u32[]{:S(2)}) copy-start(f32[512]{0:T(512)} %param.15) | copy-start | bytes 6148
  20.9 13.0 %copy-start.7 = (f32[128]{0:T(128)S(1)}, f32[128]{0:T(128)}, u32[]{:S(2)}) copy-start(f32[128]{0:T(128)} %param.14) | copy-start | bytes 1540
  20.9 5.7 %collective-permute-start.9 = (bf16[80,512]{1,0:T(8,128)(2,1)S(1)}, bf16[80,512]{1,0:T(8,128)(2,1)S(1)}, u32[]{:S(2)}, u32[]{:S(2)}) collective-permute-start(bf16[80,512]{1,0:T(8,128)(2,1)S(1)} %get-tuple-element.16), channel_id=1, source_target_pairs={{0,1},{1,0},{2,3},{3,2},{4,5},{5,4},{6,7},{7,6},{8,9},{9,8},{10,11... | collective-permute-start | bytes 245768 | tf_op jit(solution)/shard_map/ppermute | solution.py:185
  23.1 7.1 %collective-permute-start.7 = (bf16[48,512]{1,0:T(8,128)(2,1)S(1)}, bf16[48,512]{1,0:T(8,128)(2,1)S(1)}, u32[]{:S(2)}, u32[]{:S(2)}) collective-permute-start(bf16[48,512]{1,0:T(8,128)(2,1)S(1)} %get-tuple-element.13), channel_id=1, source_target_pairs={{0,2},{1,3},{2,0},{3,1},{4,6},{5,7},{6,4},{7,5},{8,10},{9,11},{10,... | collective-permute-start | bytes 147464 | tf_op jit(solution)/shard_map/ppermute | solution.py:185
  25.7 6.4 %collective-permute-start.8 = (bf16[48,512]{1,0:T(8,128)(2,1)S(1)}, bf16[48,512]{1,0:T(8,128)(2,1)S(1)}, u32[]{:S(2)}, u32[]{:S(2)}) collective-permute-start(bf16[48,512]{1,0:T(8,128)(2,1)S(1)} %get-tuple-element.14), channel_id=1, source_target_pairs={{0,3},{1,2},{2,1},{3,0},{4,7},{5,6},{6,5},{7,4},{8,11},{9,10},{10,... | collective-permute-start | bytes 147464 | tf_op jit(solution)/shard_map/ppermute | solution.py:185
  25.9 7.9 %collective-permute-start.6 = (bf16[128,512]{1,0:T(8,128)(2,1)S(1)}, bf16[128,512]{1,0:T(8,128)(2,1)S(1)}, u32[]{:S(2)}, u32[]{:S(2)}) collective-permute-start(bf16[128,512]{1,0:T(8,128)(2,1)S(1)} %get-tuple-element.12), channel_id=1, source_target_pairs={{0,1},{1,0},{2,3},{3,2},{4,5},{5,4},{6,7},{7,6},{8,9},{9,8},{10,11... | collective-permute-start | bytes 393224 | tf_op jit(solution)/shard_map/ppermute | solution.py:185
  26.6 6.8 %collective-permute-start.10 = (bf16[80,512]{1,0:T(8,128)(2,1)S(1)}, bf16[80,512]{1,0:T(8,128)(2,1)S(1)}, u32[]{:S(2)}, u32[]{:S(2)}) collective-permute-start(bf16[80,512]{1,0:T(8,128)(2,1)S(1)} %add_convert_fusion), channel_id=1, source_target_pairs={{0,2},{1,3},{2,0},{3,1},{4,6},{5,7},{6,4},{7,5},{8,10},{9,11},{10,... | collective-permute-start | bytes 245768 | tf_op jit(solution)/shard_map/ppermute | solution.py:185

commit v5 on v4

--- a/solution.py
+++ b/solution.py
@@ -18,7 +18,7 @@
         if offset:
             pairs = [(i, i - offset) for i in range(length) if 0 <= i - offset < length]
             held[offset + BAND] = lax.ppermute(ci_vector, "alpha", pairs)
-    return held, lambda block, own: block - own + BAND, ()
+    return held, lambda block, own: block - own + BAND
 
 
 def cube_window(ci_vector):
@@ -48,7 +48,7 @@
         turned = (own >= length // 2) & ((k == 1) | (k == 2))
         return jnp.where(turned, 3 - k, k)
 
-    return held, place_of, ()
+    return held, place_of
 
 
 def pick_kernel(first, last, out):
@@ -119,7 +119,7 @@
     factors, _, alpha_slots = alpha_list.shape
     _, local_blocks, beta_slots = beta_target.shape
     length, groups = lax.axis_size("alpha"), lax.axis_size("beta")
-    held, place_of, _ = window_of(length)(ci_vector)
+    held, place_of = window_of(length)(ci_vector)
     by_xor = groups & (groups - 1) == 0
     relay = groups == 4
     direct = tile_size * 3 // 8 if relay else tile_size

time: 34.9 us -> 34.9 us (level)
  no operation moved by 1% of the time
where the time goes in v5:
time: 34.9 us; the launch traced here: 34.6 us
  starting transfers between devices  15.8 us (45%)
  waiting for transfers between devices  8.54 us (24%)
  local copies, waits for them, and re-layouts  6.36 us (18%)
  Pallas kernels  2.97 us (9%)
  other arithmetic  0.85 us (2%)
    ppermute x5, starting transfers between devices, send(): return lax.ppermute(value, 'beta', pairs)  8.68 us
    unnamed x16, local copies, waits for them, and re-layouts  6.36 us
    ppermute x1, starting transfers between devices, cube_window(): lax.ppermute(ci_vector, 'alpha', [(i ^ (2 if i in lower else 1), i) for i...  3.97 us
    ppermute x5, waiting for transfers between devices, send(): return lax.ppermute(value, 'beta', pairs)  3.62 us
    ppermute x1, waiting for transfers between devices, cube_window(): lax.ppermute(ci_vector, 'alpha', [(i ^ (2 if i in lower else 1), i) for i...  3.59 us
    pallas_call x1, Pallas kernels, shards(): pl.pallas_call(body, out_shape=[jax.ShapeDtypeStruct((last - first, colum...  2.36 us
    ppermute x1, starting transfers between devices, cube_window(): held[7] = lax.ppermute(cross, 'alpha', swap)  1.96 us
    ppermute x1, waiting for transfers between devices, cube_window(): held[3] = lax.ppermute(beside, 'alpha', swap)  1.31 us
  transfers between devices with their start and end apart: 11, of which 5 were waited for; matrix products, arithmetic and copies ran while one was open for 0% of the time, Pallas kernels for 2%

profile of v5, /device:TPU:0, one launch (start us, length us, event | category | flops | bytes accessed | tf_op | source)
XLA Modules:
  0.0 34.6 jit_solution(11637026103916209086)
XLA Ops:
  0.0 0.5 %collective-permute-start.3 = (bf16[128,512]{1,0:T(8,128)(2,1)}, bf16[128,512]{1,0:T(8,128)(2,1)S(1)}, u32[]{:S(2)}, u32[]{:S(2)}) collective-permute-start(bf16[128,512]{1,0:T(8,128)(2,1)} %refs_3_.1), channel_id=1, source_target_pairs={{4,0},{0,4},{16,8},{20,12},{8,16},{12,20},{28,24},{24,28},{5,1},{1... | collective-permute-start | bytes 393224 | tf_op jit(solution)/shard_map/ppermute | solution.py:29
  0.5 4.0 %collective-permute-start.1 = (bf16[128,512]{1,0:T(8,128)(2,1)}, bf16[128,512]{1,0:T(8,128)(2,1)S(1)}, u32[]{:S(2)}, u32[]{:S(2)}) collective-permute-start(bf16[128,512]{1,0:T(8,128)(2,1)} %refs_3_.1), channel_id=1, source_target_pairs={{8,0},{12,4},{0,8},{4,12},{20,16},{16,20},{28,24},{24,28},{9,1},{1... | collective-permute-start | bytes 393224 | tf_op jit(solution)/shard_map/ppermute | solution.py:28
  4.5 0.0 collective-permute-start
  4.5 0.7 %collective-permute-start.2 = (bf16[128,512]{1,0:T(8,128)(2,1)}, bf16[128,512]{1,0:T(8,128)(2,1)S(1)}, u32[]{:S(2)}, u32[]{:S(2)}) collective-permute-start(bf16[128,512]{1,0:T(8,128)(2,1)} %refs_3_.1), channel_id=1, source_target_pairs={{16,4},{24,12},{4,16},{12,24},{17,5},{25,13},{5,17},{13,25},{18,6}... | collective-permute-start | bytes 393224 | tf_op jit(solution)/shard_map/ppermute | solution.py:31
  5.1 0.0 collective-permute-done.3.refs_7_
  5.1 2.0 %collective-permute-start.5 = (bf16[128,512]{1,0:T(8,128)(2,1)S(1)}, bf16[128,512]{1,0:T(8,128)(2,1)S(1)}, u32[]{:S(2)}, u32[]{:S(2)}) collective-permute-start(bf16[128,512]{1,0:T(8,128)(2,1)S(1)} %collective-permute-done.3.refs_7_), channel_id=1, source_target_pairs={{0,4},{4,0},{8,12},{12,8},{16,20},{20,16},{24,28},{28,24},{1,5},{5... | collective-permute-start | bytes 393224 | tf_op jit(solution)/shard_map/ppermute | solution.py:44
  7.1 3.6 %collective-permute-done.1.first.refs_5_ = bf16[128,512]{1,0:T(8,128)(2,1)S(1)} collective-permute-done((bf16[128,512]{1,0:T(8,128)(2,1)}, bf16[128,512]{1,0:T(8,128)(2,1)S(1)}, u32[]{:S(2)}, u32[]{:S(2)}) %collective-permute-start.1) | collective-permute-done | bytes 131104 | tf_op jit(solution)/shard_map/ppermute | solution.py:28
  10.7 0.0 collective-permute-done.last.refs_4_
  10.7 0.1 collective-permute-start.4
  10.8 0.0 collective-permute-done.2.refs_6_
  10.8 0.0 collective-permute-done.5.refs_9_
  10.8 1.3 %collective-permute-done.4.refs_8_ = bf16[128,512]{1,0:T(8,128)(2,1)S(1)} collective-permute-done((bf16[128,512]{1,0:T(8,128)(2,1)S(1)}, bf16[128,512]{1,0:T(8,128)(2,1)S(1)}, u32[]{:S(2)}, u32[]{:S(2)}) %collective-permute-start.4) | collective-permute-done | bytes 131104 | tf_op jit(solution)/shard_map/ppermute | solution.py:43
  12.1 0.0 copy-start
  12.1 2.2 %copy-done = bf16[8,4,4,128,128]{4,3,2,1,0:T(8,128)(2,1)S(1)} copy-done((bf16[8,4,4,128,128]{4,3,2,1,0:T(8,128)(2,1)S(1)}, bf16[8,4,4,128,128]{4,3,2,1,0:T(8,128)(2,1)}, u32[]{:S(2)}) %copy-start) | copy-done | bytes 4194328
  14.3 0.0 copy-start.1
  14.3 1.2 %copy-done.1 = bf16[8,1,4,128,128]{4,3,2,1,0:T(8,128)(2,1)S(1)} copy-done((bf16[8,1,4,128,128]{4,3,2,1,0:T(8,128)(2,1)S(1)}, bf16[8,1,4,128,128]{4,3,2,1,0:T(8,128)(2,1)}, u32[]{:S(2)}) %copy-start.1) | copy-done | bytes 1048600
  15.5 0.0 copy-start.2
  15.5 0.9 %copy-done.2 = bf16[128,512]{1,0:T(8,128)(2,1)S(1)} copy-done((bf16[128,512]{1,0:T(8,128)(2,1)S(1)}, bf16[128,512]{1,0:T(8,128)(2,1)}, u32[]{:S(2)}) %copy-start.2) | copy-done | bytes 131096
  16.4 0.0 copy-start.3
  16.4 0.7 %copy-done.3 = s32[8,4,4]{0,2,1:T(4,128)S(1)} copy-done((s32[8,4,4]{0,2,1:T(4,128)S(1)}, s32[8,4,4]{0,2,1:T(4,128)}, u32[]{:S(2)}) %copy-start.3) | copy-done | bytes 536
  17.1 0.0 copy-start.4
  17.1 0.7 %copy-done.4 = s32[8,1,4]{0,2,1:T(4,128)S(1)} copy-done((s32[8,1,4]{0,2,1:T(4,128)S(1)}, s32[8,1,4]{0,2,1:T(4,128)}, u32[]{:S(2)}) %copy-start.4) | copy-done | bytes 152
  17.8 0.0 copy-start.5
  17.8 0.7 %copy-done.5 = s32[8,1]{0,1:T(1,128)S(1)} copy-done((s32[8,1]{0,1:T(1,128)S(1)}, s32[8,1]{0,1:T(1,128)}, u32[]{:S(2)}) %copy-start.5) | copy-done | bytes 56
  18.5 2.4 %couple.1 = (bf16[128,512]{1,0:T(8,128)(2,1)S(1)}, bf16[128,512]{1,0:T(8,128)(2,1)S(1)}, bf16[48,512]{1,0:T(8,128)(2,1)S(1)}, bf16[48,512]{1,0:T(8,128)(2,1)S(1)...) custom-call(s32[1,4,8]{2,1,0:T(4,128)S(1)} %bitcast.4, s32[1,8]{1,0:T(1,128)S(1)} %bitcast.5, ...), custom_call_target="tpu_custom_call" | custom-call | flops 1073741824 | bytes 5242880 | tf_op jit(solution)/shard_map/couple/pallas_call | solution.py:156
  20.9 0.0 copy-start.6
  20.9 0.0 copy-start.7
  20.9 1.6 %collective-permute-start.9 = (bf16[80,512]{1,0:T(8,128)(2,1)S(1)}, bf16[80,512]{1,0:T(8,128)(2,1)S(1)}, u32[]{:S(2)}, u32[]{:S(2)}) collective-permute-start(bf16[80,512]{1,0:T(8,128)(2,1)S(1)} %get-tuple-element.16), channel_id=1, source_target_pairs={{0,1},{1,0},{2,3},{3,2},{4,5},{5,4},{6,7},{7,6},{8,9},{9,8},{10,11... | collective-permute-start | bytes 245768 | tf_op jit(solution)/shard_map/ppermute | solution.py:185
  22.5 0.6 %warm.1 = f32[8,128]{1,0:T(8,128)} custom-call(), custom_call_target="tpu_custom_call" | custom-call | flops 20000000000 | bytes 4096 | tf_op jit(solution)/shard_map/warm/pallas_call | solution.py:133
  23.1 2.6 %collective-permute-start.7 = (bf16[48,512]{1,0:T(8,128)(2,1)S(1)}, bf16[48,512]{1,0:T(8,128)(2,1)S(1)}, u32[]{:S(2)}, u32[]{:S(2)}) collective-permute-start(bf16[48,512]{1,0:T(8,128)(2,1)S(1)} %get-tuple-element.13), channel_id=1, source_target_pairs={{0,2},{1,3},{2,0},{3,1},{4,6},{5,7},{6,4},{7,5},{8,10},{9,11},{10,... | collective-permute-start | bytes 147464 | tf_op jit(solution)/shard_map/ppermute | solution.py:185
  25.7 0.2 collective-permute-start.8
  25.9 0.7 %collective-permute-start.6 = (bf16[128,512]{1,0:T(8,128)(2,1)S(1)}, bf16[128,512]{1,0:T(8,128)(2,1)S(1)}, u32[]{:S(2)}, u32[]{:S(2)}) collective-permute-start(bf16[128,512]{1,0:T(8,128)(2,1)S(1)} %get-tuple-element.12), channel_id=1, source_target_pairs={{0,1},{1,0},{2,3},{3,2},{4,5},{5,4},{6,7},{7,6},{8,9},{9,8},{10,11... | collective-permute-start | bytes 393224 | tf_op jit(solution)/shard_map/ppermute | solution.py:185
  26.6 0.0 collective-permute-done.9
  26.6 3.6 %collective-permute-start.10 = (bf16[80,512]{1,0:T(8,128)(2,1)S(1)}, bf16[80,512]{1,0:T(8,128)(2,1)S(1)}, u32[]{:S(2)}, u32[]{:S(2)}) collective-permute-start(bf16[80,512]{1,0:T(8,128)(2,1)S(1)} %add_convert_fusion), channel_id=1, source_target_pairs={{0,2},{1,3},{2,0},{3,1},{4,6},{5,7},{6,4},{7,5},{8,10},{9,11},{10,... | collective-permute-start | bytes 245768 | tf_op jit(solution)/shard_map/ppermute | solution.py:185
  30.2 0.0 collective-permute-done.7
  30.2 1.9 %collective-permute-done.8 = bf16[48,512]{1,0:T(8,128)(2,1)S(1)} collective-permute-done((bf16[48,512]{1,0:T(8,128)(2,1)S(1)}, bf16[48,512]{1,0:T(8,128)(2,1)S(1)}, u32[]{:S(2)}, u32[]{:S(2)}) %collective-permute-start.8) | collective-permute-done | bytes 49184 | tf_op jit(solution)/shard_map/ppermute | solution.py:185
  32.1 1.3 %collective-permute-done.10 = bf16[80,512]{1,0:T(8,128)(2,1)S(1)} collective-permute-done((bf16[80,512]{1,0:T(8,128)(2,1)S(1)}, bf16[80,512]{1,0:T(8,128)(2,1)S(1)}, u32[]{:S(2)}, u32[]{:S(2)}) %collective-permute-start.10) | collective-permute-done | bytes 81952 | tf_op jit(solution)/shard_map/ppermute | solution.py:185
  33.4 0.4 %collective-permute-done.6 = bf16[128,512]{1,0:T(8,128)(2,1)S(1)} collective-permute-done((bf16[128,512]{1,0:T(8,128)(2,1)S(1)}, bf16[128,512]{1,0:T(8,128)(2,1)S(1)}, u32[]{:S(2)}, u32[]{:S(2)}) %collective-permute-start.6) | collective-permute-done | bytes 131104 | tf_op jit(solution)/shard_map/ppermute | solution.py:185
  33.8 0.0 copy-done.6
  33.8 0.0 copy-done.7
  33.8 0.8 %fusion.1 = f32[128,512]{1,0:T(8,128)} fusion(f32[80,512]{1,0:T(8,128)S(1)} %convert_element_type.34, f32[48,512]{1,0:T(8,128)S(1)} %convert_add_fusion, bf16[128,512]{1,0:T(8,128)(2,1)S(1)} %copy-done.2, bf16[128,512]{1,0:T(8,128)(2,1)S(1)} %collective-permute-done.6, bf16[128,512]{1,0:T(8,128)(2,1)S(1)} %get-tuple-element.11, f32[512]{0:T(512)S(1)} %copy-done.6, ...), kind=kLoop, calls=%fused_computation.2 | loop fusion | flops 589824 | bytes 920064 | tf_op jit(solution)/shard_map/add | solution.py:194
  (4 shorter events, 0.1 us)
Async XLA Ops:
  0.0 5.1 %collective-permute-start.3 = (bf16[128,512]{1,0:T(8,128)(2,1)}, bf16[128,512]{1,0:T(8,128)(2,1)S(1)}, u32[]{:S(2)}, u32[]{:S(2)}) collective-permute-start(bf16[128,512]{1,0:T(8,128)(2,1)} %refs_3_.1), channel_id=1, source_target_pairs={{4,0},{0,4},{16,8},{20,12},{8,16},{12,20},{28,24},{24,28},{5,1},{1... | collective-permute-start | bytes 393224 | tf_op jit(solution)/shard_map/ppermute | solution.py:29
  0.5 10.2 %collective-permute-start.1 = (bf16[128,512]{1,0:T(8,128)(2,1)}, bf16[128,512]{1,0:T(8,128)(2,1)S(1)}, u32[]{:S(2)}, u32[]{:S(2)}) collective-permute-start(bf16[128,512]{1,0:T(8,128)(2,1)} %refs_3_.1), channel_id=1, source_target_pairs={{8,0},{12,4},{0,8},{4,12},{20,16},{16,20},{28,24},{24,28},{9,1},{1... | collective-permute-start | bytes 393224 | tf_op jit(solution)/shard_map/ppermute | solution.py:28
  4.5 6.2 %collective-permute-start = (bf16[128,512]{1,0:T(8,128)(2,1)}, bf16[128,512]{1,0:T(8,128)(2,1)S(1)}, u32[]{:S(2)}, u32[]{:S(2)}) collective-permute-start(bf16[128,512]{1,0:T(8,128)(2,1)} %refs_3_.1), channel_id=1, source_target_pairs={{4,0},{0,4},{12,8},{8,12},{24,16},{28,20},{16,24},{20,28},{5,1},{1... | collective-permute-start | bytes 393224 | tf_op jit(solution)/shard_map/ppermute | solution.py:30
  4.5 6.3 %collective-permute-start.2 = (bf16[128,512]{1,0:T(8,128)(2,1)}, bf16[128,512]{1,0:T(8,128)(2,1)S(1)}, u32[]{:S(2)}, u32[]{:S(2)}) collective-permute-start(bf16[128,512]{1,0:T(8,128)(2,1)} %refs_3_.1), channel_id=1, source_target_pairs={{16,4},{24,12},{4,16},{12,24},{17,5},{25,13},{5,17},{13,25},{18,6}... | collective-permute-start | bytes 393224 | tf_op jit(solution)/shard_map/ppermute | solution.py:31
  5.1 5.7 %collective-permute-start.5 = (bf16[128,512]{1,0:T(8,128)(2,1)S(1)}, bf16[128,512]{1,0:T(8,128)(2,1)S(1)}, u32[]{:S(2)}, u32[]{:S(2)}) collective-permute-start(bf16[128,512]{1,0:T(8,128)(2,1)S(1)} %collective-permute-done.3.refs_7_), channel_id=1, source_target_pairs={{0,4},{4,0},{8,12},{12,8},{16,20},{20,16},{24,28},{28,24},{1,5},{5... | collective-permute-start | bytes 393224 | tf_op jit(solution)/shard_map/ppermute | solution.py:44
  10.7 1.4 %collective-permute-start.4 = (bf16[128,512]{1,0:T(8,128)(2,1)S(1)}, bf16[128,512]{1,0:T(8,128)(2,1)S(1)}, u32[]{:S(2)}, u32[]{:S(2)}) collective-permute-start(bf16[128,512]{1,0:T(8,128)(2,1)S(1)} %pick.1), channel_id=1, source_target_pairs={{0,4},{4,0},{8,12},{12,8},{16,20},{20,16},{24,28},{28,24},{1,5},{5... | collective-permute-start | bytes 393224 | tf_op jit(solution)/shard_map/ppermute | solution.py:43
  12.1 2.2 %copy-start = (bf16[8,4,4,128,128]{4,3,2,1,0:T(8,128)(2,1)S(1)}, bf16[8,4,4,128,128]{4,3,2,1,0:T(8,128)(2,1)}, u32[]{:S(2)}) copy-start(bf16[8,4,4,128,128]{4,3,2,1,0:T(8,128)(2,1)} %refs_11_.1) | copy-start | bytes 12582916
  14.3 1.2 %copy-start.1 = (bf16[8,1,4,128,128]{4,3,2,1,0:T(8,128)(2,1)S(1)}, bf16[8,1,4,128,128]{4,3,2,1,0:T(8,128)(2,1)}, u32[]{:S(2)}) copy-start(bf16[8,1,4,128,128]{4,3,2,1,0:T(8,128)(2,1)} %refs_10_.1) | copy-start | bytes 3145732
  15.5 0.9 %copy-start.2 = (bf16[128,512]{1,0:T(8,128)(2,1)S(1)}, bf16[128,512]{1,0:T(8,128)(2,1)}, u32[]{:S(2)}) copy-start(bf16[128,512]{1,0:T(8,128)(2,1)} %refs_3_.1) | copy-start | bytes 393220
  16.4 0.7 %copy-start.3 = (s32[8,4,4]{0,2,1:T(4,128)S(1)}, s32[8,4,4]{0,2,1:T(4,128)}, u32[]{:S(2)}) copy-start(s32[8,4,4]{0,2,1:T(4,128)} %param.13) | copy-start | bytes 1540
  17.1 0.7 %copy-start.4 = (s32[8,1,4]{0,2,1:T(4,128)S(1)}, s32[8,1,4]{0,2,1:T(4,128)}, u32[]{:S(2)}) copy-start(s32[8,1,4]{0,2,1:T(4,128)} %param.10) | copy-start | bytes 388
  17.8 0.7 %copy-start.5 = (s32[8,1]{0,1:T(1,128)S(1)}, s32[8,1]{0,1:T(1,128)}, u32[]{:S(2)}) copy-start(s32[8,1]{0,1:T(1,128)} %param.11) | copy-start | bytes 100
  20.9 13.0 %copy-start.6 = (f32[512]{0:T(512)S(1)}, f32[512]{0:T(512)}, u32[]{:S(2)}) copy-start(f32[512]{0:T(512)} %param.15) | copy-start | bytes 6148
  20.9 13.0 %copy-start.7 = (f32[128]{0:T(128)S(1)}, f32[128]{0:T(128)}, u32[]{:S(2)}) copy-start(f32[128]{0:T(128)} %param.14) | copy-start | bytes 1540
  20.9 5.7 %collective-permute-start.9 = (bf16[80,512]{1,0:T(8,128)(2,1)S(1)}, bf16[80,512]{1,0:T(8,128)(2,1)S(1)}, u32[]{:S(2)}, u32[]{:S(2)}) collective-permute-start(bf16[80,512]{1,0:T(8,128)(2,1)S(1)} %get-tuple-element.16), channel_id=1, source_target_pairs={{0,1},{1,0},{2,3},{3,2},{4,5},{5,4},{6,7},{7,6},{8,9},{9,8},{10,11... | collective-permute-start | bytes 245768 | tf_op jit(solution)/shard_map/ppermute | solution.py:185
  23.1 7.1 %collective-permute-start.7 = (bf16[48,512]{1,0:T(8,128)(2,1)S(1)}, bf16[48,512]{1,0:T(8,128)(2,1)S(1)}, u32[]{:S(2)}, u32[]{:S(2)}) collective-permute-start(bf16[48,512]{1,0:T(8,128)(2,1)S(1)} %get-tuple-element.13), channel_id=1, source_target_pairs={{0,2},{1,3},{2,0},{3,1},{4,6},{5,7},{6,4},{7,5},{8,10},{9,11},{10,... | collective-permute-start | bytes 147464 | tf_op jit(solution)/shard_map/ppermute | solution.py:185
  25.7 6.4 %collective-permute-start.8 = (bf16[48,512]{1,0:T(8,128)(2,1)S(1)}, bf16[48,512]{1,0:T(8,128)(2,1)S(1)}, u32[]{:S(2)}, u32[]{:S(2)}) collective-permute-start(bf16[48,512]{1,0:T(8,128)(2,1)S(1)} %get-tuple-element.14), channel_id=1, source_target_pairs={{0,3},{1,2},{2,1},{3,0},{4,7},{5,6},{6,5},{7,4},{8,11},{9,10},{10,... | collective-permute-start | bytes 147464 | tf_op jit(solution)/shard_map/ppermute | solution.py:185
  25.9 7.9 %collective-permute-start.6 = (bf16[128,512]{1,0:T(8,128)(2,1)S(1)}, bf16[128,512]{1,0:T(8,128)(2,1)S(1)}, u32[]{:S(2)}, u32[]{:S(2)}) collective-permute-start(bf16[128,512]{1,0:T(8,128)(2,1)S(1)} %get-tuple-element.12), channel_id=1, source_target_pairs={{0,1},{1,0},{2,3},{3,2},{4,5},{5,4},{6,7},{7,6},{8,9},{9,8},{10,11... | collective-permute-start | bytes 393224 | tf_op jit(solution)/shard_map/ppermute | solution.py:185
  26.6 6.8 %collective-permute-start.10 = (bf16[80,512]{1,0:T(8,128)(2,1)S(1)}, bf16[80,512]{1,0:T(8,128)(2,1)S(1)}, u32[]{:S(2)}, u32[]{:S(2)}) collective-permute-start(bf16[80,512]{1,0:T(8,128)(2,1)S(1)} %add_convert_fusion), channel_id=1, source_target_pairs={{0,2},{1,3},{2,0},{3,1},{4,6},{5,7},{6,4},{7,5},{8,10},{9,11},{10,... | collective-permute-start | bytes 245768 | tf_op jit(solution)/shard_map/ppermute | solution.py:185

commit v6 on v5

--- a/solution.py
+++ b/solution.py
@@ -122,10 +122,11 @@
     held, place_of = window_of(length)(ci_vector)
     by_xor = groups & (groups - 1) == 0
     relay = groups == 4
-    direct = tile_size * 3 // 8 if relay else tile_size
-    parts = [(away, 0, tile_size if away < 2 else direct) for away in range(groups)]
+    parts = [(away, 0, tile_size) for away in range(groups)]
     if relay:
-        parts += [(away, direct, tile_size) for away in (2, 3)]
+        early, direct = tile_size * 13 // 16, tile_size * 5 // 16
+        parts[1:] = [(1, 0, early), (2, 0, direct), (3, 0, direct)]
+        parts += [(1, early, tile_size), (2, direct, tile_size), (3, direct, tile_size)]
     sizes = (factors, alpha_slots, local_blocks, beta_slots, groups, by_xor, parts)
     vmem = pl.BlockSpec(memory_space=pltpu.VMEM)
     tile_bytes = (alpha_tiles.size + beta_tiles.size) * 2
@@ -189,6 +190,8 @@
         beyond = send(far[-1], 1)
         joined = (far[-2].astype(jnp.float32) + beyond.astype(jnp.float32)).astype(jnp.bfloat16)
         passed = send(joined, 2).astype(jnp.float32)
+        rest = send(far[-3], 1).astype(jnp.float32)
+        received[0] = jnp.concatenate([received[0], rest], axis=0)
         received[1:] = [jnp.concatenate([received[1] + received[2], passed], axis=0)]
     summed = own.astype(jnp.float32) + sum(received)
     return summed + (alpha_diag[:, None] + beta_diag[None, :]) * ci_vector.astype(jnp.float32)

time: 34.9 us -> 36.2 us (1.037)
  waiting for transfers between devices: 8.54 us -> 9.37 us
  starting transfers between devices: 15.8 us -> 16.3 us
    ppermute x5 -> x6, waiting for transfers between devices: 3.62 us -> 4.45 us  [send(): return lax.ppermute(value, 'beta', pairs)]
    ppermute x5 -> x6, starting transfers between devices: 8.68 us -> 9.13 us  [send(): return lax.ppermute(value, 'beta', pairs)]
  transfers between devices with their start and end apart: 11 -> 12, of which waited for: 5 -> 4; matrix products, arithmetic and copies ran while one was open for 0% -> 0% of each run, Pallas kernels for 2% -> 2%
where the time goes in v6:
time: 36.2 us; the launch traced here: 36 us
  starting transfers between devices  16.3 us (45%)
  waiting for transfers between devices  9.37 us (26%)
  local copies, waits for them, and re-layouts  6.36 us (18%)
  Pallas kernels  2.96 us (8%)
  other arithmetic  0.86 us (2%)
    ppermute x6, starting transfers between devices, send(): return lax.ppermute(value, 'beta', pairs)  9.13 us
    unnamed x16, local copies, waits for them, and re-layouts  6.36 us
    ppermute x6, waiting for transfers between devices, send(): return lax.ppermute(value, 'beta', pairs)  4.45 us
    ppermute x1, starting transfers between devices, cube_window(): lax.ppermute(ci_vector, 'alpha', [(i ^ (2 if i in lower else 1), i) for i...  3.97 us
    ppermute x1, waiting for transfers between devices, cube_window(): lax.ppermute(ci_vector, 'alpha', [(i ^ (2 if i in lower else 1), i) for i...  3.59 us
    pallas_call x1, Pallas kernels, shards(): pl.pallas_call(body, out_shape=[jax.ShapeDtypeStruct((last - first, colum...  2.36 us
    ppermute x1, starting transfers between devices, cube_window(): held[7] = lax.ppermute(cross, 'alpha', swap)  1.96 us
    ppermute x1, waiting for transfers between devices, cube_window(): held[3] = lax.ppermute(beside, 'alpha', swap)  1.31 us
  transfers between devices with their start and end apart: 12, of which 4 were waited for; matrix products, arithmetic and copies ran while one was open for 0% of the time, Pallas kernels for 2%

profile of v6, /device:TPU:0, one launch (start us, length us, event | category | flops | bytes accessed | tf_op | source)
XLA Modules:
  0.0 36.0 jit_solution(4327506747948885392)
XLA Ops:
  0.0 0.5 %collective-permute-start.3 = (bf16[128,512]{1,0:T(8,128)(2,1)}, bf16[128,512]{1,0:T(8,128)(2,1)S(1)}, u32[]{:S(2)}, u32[]{:S(2)}) collective-permute-start(bf16[128,512]{1,0:T(8,128)(2,1)} %refs_3_.1), channel_id=1, source_target_pairs={{4,0},{0,4},{16,8},{20,12},{8,16},{12,20},{28,24},{24,28},{5,1},{1... | collective-permute-start | bytes 393224 | tf_op jit(solution)/shard_map/ppermute | solution.py:29
  0.5 4.0 %collective-permute-start.1 = (bf16[128,512]{1,0:T(8,128)(2,1)}, bf16[128,512]{1,0:T(8,128)(2,1)S(1)}, u32[]{:S(2)}, u32[]{:S(2)}) collective-permute-start(bf16[128,512]{1,0:T(8,128)(2,1)} %refs_3_.1), channel_id=1, source_target_pairs={{8,0},{12,4},{0,8},{4,12},{20,16},{16,20},{28,24},{24,28},{9,1},{1... | collective-permute-start | bytes 393224 | tf_op jit(solution)/shard_map/ppermute | solution.py:28
  4.5 0.0 collective-permute-start
  4.5 0.7 %collective-permute-start.2 = (bf16[128,512]{1,0:T(8,128)(2,1)}, bf16[128,512]{1,0:T(8,128)(2,1)S(1)}, u32[]{:S(2)}, u32[]{:S(2)}) collective-permute-start(bf16[128,512]{1,0:T(8,128)(2,1)} %refs_3_.1), channel_id=1, source_target_pairs={{16,4},{24,12},{4,16},{12,24},{17,5},{25,13},{5,17},{13,25},{18,6}... | collective-permute-start | bytes 393224 | tf_op jit(solution)/shard_map/ppermute | solution.py:31
  5.1 0.0 collective-permute-done.3.refs_7_
  5.1 2.0 %collective-permute-start.5 = (bf16[128,512]{1,0:T(8,128)(2,1)S(1)}, bf16[128,512]{1,0:T(8,128)(2,1)S(1)}, u32[]{:S(2)}, u32[]{:S(2)}) collective-permute-start(bf16[128,512]{1,0:T(8,128)(2,1)S(1)} %collective-permute-done.3.refs_7_), channel_id=1, source_target_pairs={{0,4},{4,0},{8,12},{12,8},{16,20},{20,16},{24,28},{28,24},{1,5},{5... | collective-permute-start | bytes 393224 | tf_op jit(solution)/shard_map/ppermute | solution.py:44
  7.1 3.6 %collective-permute-done.1.first.refs_5_ = bf16[128,512]{1,0:T(8,128)(2,1)S(1)} collective-permute-done((bf16[128,512]{1,0:T(8,128)(2,1)}, bf16[128,512]{1,0:T(8,128)(2,1)S(1)}, u32[]{:S(2)}, u32[]{:S(2)}) %collective-permute-start.1) | collective-permute-done | bytes 131104 | tf_op jit(solution)/shard_map/ppermute | solution.py:28
  10.7 0.0 collective-permute-done.last.refs_4_
  10.7 0.1 collective-permute-start.4
  10.8 0.0 collective-permute-done.2.refs_6_
  10.8 0.0 collective-permute-done.5.refs_9_
  10.8 1.3 %collective-permute-done.4.refs_8_ = bf16[128,512]{1,0:T(8,128)(2,1)S(1)} collective-permute-done((bf16[128,512]{1,0:T(8,128)(2,1)S(1)}, bf16[128,512]{1,0:T(8,128)(2,1)S(1)}, u32[]{:S(2)}, u32[]{:S(2)}) %collective-permute-start.4) | collective-permute-done | bytes 131104 | tf_op jit(solution)/shard_map/ppermute | solution.py:43
  12.1 0.0 copy-start
  12.1 2.2 %copy-done = bf16[8,4,4,128,128]{4,3,2,1,0:T(8,128)(2,1)S(1)} copy-done((bf16[8,4,4,128,128]{4,3,2,1,0:T(8,128)(2,1)S(1)}, bf16[8,4,4,128,128]{4,3,2,1,0:T(8,128)(2,1)}, u32[]{:S(2)}) %copy-start) | copy-done | bytes 4194328
  14.3 0.0 copy-start.1
  14.3 1.2 %copy-done.1 = bf16[8,1,4,128,128]{4,3,2,1,0:T(8,128)(2,1)S(1)} copy-done((bf16[8,1,4,128,128]{4,3,2,1,0:T(8,128)(2,1)S(1)}, bf16[8,1,4,128,128]{4,3,2,1,0:T(8,128)(2,1)}, u32[]{:S(2)}) %copy-start.1) | copy-done | bytes 1048600
  15.5 0.0 copy-start.2
  15.5 0.9 %copy-done.2 = bf16[128,512]{1,0:T(8,128)(2,1)S(1)} copy-done((bf16[128,512]{1,0:T(8,128)(2,1)S(1)}, bf16[128,512]{1,0:T(8,128)(2,1)}, u32[]{:S(2)}) %copy-start.2) | copy-done | bytes 131096
  16.4 0.0 copy-start.3
  16.4 0.7 %copy-done.3 = s32[8,4,4]{0,2,1:T(4,128)S(1)} copy-done((s32[8,4,4]{0,2,1:T(4,128)S(1)}, s32[8,4,4]{0,2,1:T(4,128)}, u32[]{:S(2)}) %copy-start.3) | copy-done | bytes 536
  17.1 0.0 copy-start.4
  17.1 0.7 %copy-done.4 = s32[8,1,4]{0,2,1:T(4,128)S(1)} copy-done((s32[8,1,4]{0,2,1:T(4,128)S(1)}, s32[8,1,4]{0,2,1:T(4,128)}, u32[]{:S(2)}) %copy-start.4) | copy-done | bytes 152
  17.8 0.0 copy-start.5
  17.8 0.7 %copy-done.5 = s32[8,1]{0,1:T(1,128)S(1)} copy-done((s32[8,1]{0,1:T(1,128)S(1)}, s32[8,1]{0,1:T(1,128)}, u32[]{:S(2)}) %copy-start.5) | copy-done | bytes 56
  18.5 2.4 %couple.1 = (bf16[128,512]{1,0:T(8,128)(2,1)S(1)}, bf16[104,512]{1,0:T(8,128)(2,1)S(1)}, bf16[40,512]{1,0:T(8,128)(2,1)S(1)}, bf16[40,512]{1,0:T(8,128)(2,1)S(1)...) custom-call(s32[1,4,8]{2,1,0:T(4,128)S(1)} %bitcast.4, ...), custom_call_target="tpu_custom_call" | custom-call | flops 1073741824 | bytes 5242880 | tf_op jit(solution)/shard_map/couple/pallas_call | solution.py:157
  20.8 0.0 copy-start.6
  20.9 0.0 copy-start.7
  20.9 1.6 %collective-permute-start.10 = (bf16[88,512]{1,0:T(8,128)(2,1)S(1)}, bf16[88,512]{1,0:T(8,128)(2,1)S(1)}, u32[]{:S(2)}, u32[]{:S(2)}) collective-permute-start(bf16[88,512]{1,0:T(8,128)(2,1)S(1)} %get-tuple-element.18), channel_id=1, source_target_pairs={{0,1},{1,0},{2,3},{3,2},{4,5},{5,4},{6,7},{7,6},{8,9},{9,8},{10,11... | collective-permute-start | bytes 270344 | tf_op jit(solution)/shard_map/ppermute | solution.py:186
  22.5 0.6 %warm.1 = f32[8,128]{1,0:T(8,128)} custom-call(), custom_call_target="tpu_custom_call" | custom-call | flops 20000000000 | bytes 4096 | tf_op jit(solution)/shard_map/warm/pallas_call | solution.py:134
  23.1 0.5 %collective-permute-start.7 = (bf16[24,512]{1,0:T(8,128)(2,1)S(1)}, bf16[24,512]{1,0:T(8,128)(2,1)S(1)}, u32[]{:S(2)}, u32[]{:S(2)}) collective-permute-start(bf16[24,512]{1,0:T(8,128)(2,1)S(1)} %get-tuple-element.14), channel_id=1, source_target_pairs={{0,1},{1,0},{2,3},{3,2},{4,5},{5,4},{6,7},{7,6},{8,9},{9,8},{10,11... | collective-permute-start | bytes 73736 | tf_op jit(solution)/shard_map/ppermute | solution.py:186
  23.6 2.6 %collective-permute-start.8 = (bf16[40,512]{1,0:T(8,128)(2,1)S(1)}, bf16[40,512]{1,0:T(8,128)(2,1)S(1)}, u32[]{:S(2)}, u32[]{:S(2)}) collective-permute-start(bf16[40,512]{1,0:T(8,128)(2,1)S(1)} %get-tuple-element.15), channel_id=1, source_target_pairs={{0,2},{1,3},{2,0},{3,1},{4,6},{5,7},{6,4},{7,5},{8,10},{9,11},{10,... | collective-permute-start | bytes 122888 | tf_op jit(solution)/shard_map/ppermute | solution.py:186
  26.1 1.3 %collective-permute-start.9 = (bf16[40,512]{1,0:T(8,128)(2,1)S(1)}, bf16[40,512]{1,0:T(8,128)(2,1)S(1)}, u32[]{:S(2)}, u32[]{:S(2)}) collective-permute-start(bf16[40,512]{1,0:T(8,128)(2,1)S(1)} %get-tuple-element.16), channel_id=1, source_target_pairs={{0,3},{1,2},{2,1},{3,0},{4,7},{5,6},{6,5},{7,4},{8,11},{9,10},{10,... | collective-permute-start | bytes 122888 | tf_op jit(solution)/shard_map/ppermute | solution.py:186
  27.5 0.2 collective-permute-start.6
  27.7 0.0 collective-permute-done.10
  27.8 2.9 %collective-permute-start.11 = (bf16[88,512]{1,0:T(8,128)(2,1)S(1)}, bf16[88,512]{1,0:T(8,128)(2,1)S(1)}, u32[]{:S(2)}, u32[]{:S(2)}) collective-permute-start(bf16[88,512]{1,0:T(8,128)(2,1)S(1)} %add_convert_fusion), channel_id=1, source_target_pairs={{0,2},{1,3},{2,0},{3,1},{4,6},{5,7},{6,4},{7,5},{8,10},{9,11},{10,... | collective-permute-start | bytes 270344 | tf_op jit(solution)/shard_map/ppermute | solution.py:186
  30.6 0.0 collective-permute-done.8
  30.6 1.9 %collective-permute-done.9 = bf16[40,512]{1,0:T(8,128)(2,1)S(1)} collective-permute-done((bf16[40,512]{1,0:T(8,128)(2,1)S(1)}, bf16[40,512]{1,0:T(8,128)(2,1)S(1)}, u32[]{:S(2)}, u32[]{:S(2)}) %collective-permute-start.9) | collective-permute-done | bytes 40992 | tf_op jit(solution)/shard_map/ppermute | solution.py:186
  32.5 2.6 %collective-permute-done.11 = bf16[88,512]{1,0:T(8,128)(2,1)S(1)} collective-permute-done((bf16[88,512]{1,0:T(8,128)(2,1)S(1)}, bf16[88,512]{1,0:T(8,128)(2,1)S(1)}, u32[]{:S(2)}, u32[]{:S(2)}) %collective-permute-start.11) | collective-permute-done | bytes 90144 | tf_op jit(solution)/shard_map/ppermute | solution.py:186
  35.1 0.0 collective-permute-done.7
  35.1 0.0 collective-permute-done.6
  35.1 0.0 copy-done.6
  35.1 0.0 copy-done.7
  35.1 0.8 %fusion.1 = f32[128,512]{1,0:T(8,128)} fusion(f32[88,512]{1,0:T(8,128)S(1)} %convert_element_type.32, f32[40,512]{1,0:T(8,128)S(1)} %convert_add_fusion, bf16[128,512]{1,0:T(8,128)(2,1)S(1)} %copy-done.2, bf16[128,512]{1,0:T(8,128)(2,1)S(1)} %get-tuple-element.12, bf16[24,512]{1,0:T(8,128)(2,1)S(1)} %collective-permute-done.7, ...), kind=kLoop, calls=%fused_computation.2 | loop fusion | flops 786432 | bytes 920064 | tf_op jit(solution)/shard_map/add | solution.py:197
  (4 shorter events, 0.1 us)
Async XLA Ops:
  0.0 5.1 %collective-permute-start.3 = (bf16[128,512]{1,0:T(8,128)(2,1)}, bf16[128,512]{1,0:T(8,128)(2,1)S(1)}, u32[]{:S(2)}, u32[]{:S(2)}) collective-permute-start(bf16[128,512]{1,0:T(8,128)(2,1)} %refs_3_.1), channel_id=1, source_target_pairs={{4,0},{0,4},{16,8},{20,12},{8,16},{12,20},{28,24},{24,28},{5,1},{1... | collective-permute-start | bytes 393224 | tf_op jit(solution)/shard_map/ppermute | solution.py:29
  0.5 10.2 %collective-permute-start.1 = (bf16[128,512]{1,0:T(8,128)(2,1)}, bf16[128,512]{1,0:T(8,128)(2,1)S(1)}, u32[]{:S(2)}, u32[]{:S(2)}) collective-permute-start(bf16[128,512]{1,0:T(8,128)(2,1)} %refs_3_.1), channel_id=1, source_target_pairs={{8,0},{12,4},{0,8},{4,12},{20,16},{16,20},{28,24},{24,28},{9,1},{1... | collective-permute-start | bytes 393224 | tf_op jit(solution)/shard_map/ppermute | solution.py:28
  4.5 6.2 %collective-permute-start = (bf16[128,512]{1,0:T(8,128)(2,1)}, bf16[128,512]{1,0:T(8,128)(2,1)S(1)}, u32[]{:S(2)}, u32[]{:S(2)}) collective-permute-start(bf16[128,512]{1,0:T(8,128)(2,1)} %refs_3_.1), channel_id=1, source_target_pairs={{4,0},{0,4},{12,8},{8,12},{24,16},{28,20},{16,24},{20,28},{5,1},{1... | collective-permute-start | bytes 393224 | tf_op jit(solution)/shard_map/ppermute | solution.py:30
  4.5 6.3 %collective-permute-start.2 = (bf16[128,512]{1,0:T(8,128)(2,1)}, bf16[128,512]{1,0:T(8,128)(2,1)S(1)}, u32[]{:S(2)}, u32[]{:S(2)}) collective-permute-start(bf16[128,512]{1,0:T(8,128)(2,1)} %refs_3_.1), channel_id=1, source_target_pairs={{16,4},{24,12},{4,16},{12,24},{17,5},{25,13},{5,17},{13,25},{18,6}... | collective-permute-start | bytes 393224 | tf_op jit(solution)/shard_map/ppermute | solution.py:31
  5.1 5.7 %collective-permute-start.5 = (bf16[128,512]{1,0:T(8,128)(2,1)S(1)}, bf16[128,512]{1,0:T(8,128)(2,1)S(1)}, u32[]{:S(2)}, u32[]{:S(2)}) collective-permute-start(bf16[128,512]{1,0:T(8,128)(2,1)S(1)} %collective-permute-done.3.refs_7_), channel_id=1, source_target_pairs={{0,4},{4,0},{8,12},{12,8},{16,20},{20,16},{24,28},{28,24},{1,5},{5... | collective-permute-start | bytes 393224 | tf_op jit(solution)/shard_map/ppermute | solution.py:44
  10.7 1.4 %collective-permute-start.4 = (bf16[128,512]{1,0:T(8,128)(2,1)S(1)}, bf16[128,512]{1,0:T(8,128)(2,1)S(1)}, u32[]{:S(2)}, u32[]{:S(2)}) collective-permute-start(bf16[128,512]{1,0:T(8,128)(2,1)S(1)} %pick.1), channel_id=1, source_target_pairs={{0,4},{4,0},{8,12},{12,8},{16,20},{20,16},{24,28},{28,24},{1,5},{5... | collective-permute-start | bytes 393224 | tf_op jit(solution)/shard_map/ppermute | solution.py:43
  12.1 2.2 %copy-start = (bf16[8,4,4,128,128]{4,3,2,1,0:T(8,128)(2,1)S(1)}, bf16[8,4,4,128,128]{4,3,2,1,0:T(8,128)(2,1)}, u32[]{:S(2)}) copy-start(bf16[8,4,4,128,128]{4,3,2,1,0:T(8,128)(2,1)} %refs_11_.1) | copy-start | bytes 12582916
  14.3 1.2 %copy-start.1 = (bf16[8,1,4,128,128]{4,3,2,1,0:T(8,128)(2,1)S(1)}, bf16[8,1,4,128,128]{4,3,2,1,0:T(8,128)(2,1)}, u32[]{:S(2)}) copy-start(bf16[8,1,4,128,128]{4,3,2,1,0:T(8,128)(2,1)} %refs_10_.1) | copy-start | bytes 3145732
  15.5 0.9 %copy-start.2 = (bf16[128,512]{1,0:T(8,128)(2,1)S(1)}, bf16[128,512]{1,0:T(8,128)(2,1)}, u32[]{:S(2)}) copy-start(bf16[128,512]{1,0:T(8,128)(2,1)} %refs_3_.1) | copy-start | bytes 393220
  16.4 0.7 %copy-start.3 = (s32[8,4,4]{0,2,1:T(4,128)S(1)}, s32[8,4,4]{0,2,1:T(4,128)}, u32[]{:S(2)}) copy-start(s32[8,4,4]{0,2,1:T(4,128)} %param.13) | copy-start | bytes 1540
  17.1 0.7 %copy-start.4 = (s32[8,1,4]{0,2,1:T(4,128)S(1)}, s32[8,1,4]{0,2,1:T(4,128)}, u32[]{:S(2)}) copy-start(s32[8,1,4]{0,2,1:T(4,128)} %param.10) | copy-start | bytes 388
  17.8 0.7 %copy-start.5 = (s32[8,1]{0,1:T(1,128)S(1)}, s32[8,1]{0,1:T(1,128)}, u32[]{:S(2)}) copy-start(s32[8,1]{0,1:T(1,128)} %param.11) | copy-start | bytes 100
  20.8 14.3 %copy-start.6 = (f32[512]{0:T(512)S(1)}, f32[512]{0:T(512)}, u32[]{:S(2)}) copy-start(f32[512]{0:T(512)} %param.15) | copy-start | bytes 6148
  20.9 14.3 %copy-start.7 = (f32[128]{0:T(128)S(1)}, f32[128]{0:T(128)}, u32[]{:S(2)}) copy-start(f32[128]{0:T(128)} %param.14) | copy-start | bytes 1540
  20.9 6.9 %collective-permute-start.10 = (bf16[88,512]{1,0:T(8,128)(2,1)S(1)}, bf16[88,512]{1,0:T(8,128)(2,1)S(1)}, u32[]{:S(2)}, u32[]{:S(2)}) collective-permute-start(bf16[88,512]{1,0:T(8,128)(2,1)S(1)} %get-tuple-element.18), channel_id=1, source_target_pairs={{0,1},{1,0},{2,3},{3,2},{4,5},{5,4},{6,7},{7,6},{8,9},{9,8},{10,11... | collective-permute-start | bytes 270344 | tf_op jit(solution)/shard_map/ppermute | solution.py:186
  23.1 12.0 %collective-permute-start.7 = (bf16[24,512]{1,0:T(8,128)(2,1)S(1)}, bf16[24,512]{1,0:T(8,128)(2,1)S(1)}, u32[]{:S(2)}, u32[]{:S(2)}) collective-permute-start(bf16[24,512]{1,0:T(8,128)(2,1)S(1)} %get-tuple-element.14), channel_id=1, source_target_pairs={{0,1},{1,0},{2,3},{3,2},{4,5},{5,4},{6,7},{7,6},{8,9},{9,8},{10,11... | collective-permute-start | bytes 73736 | tf_op jit(solution)/shard_map/ppermute | solution.py:186
  23.6 7.1 %collective-permute-start.8 = (bf16[40,512]{1,0:T(8,128)(2,1)S(1)}, bf16[40,512]{1,0:T(8,128)(2,1)S(1)}, u32[]{:S(2)}, u32[]{:S(2)}) collective-permute-start(bf16[40,512]{1,0:T(8,128)(2,1)S(1)} %get-tuple-element.15), channel_id=1, source_target_pairs={{0,2},{1,3},{2,0},{3,1},{4,6},{5,7},{6,4},{7,5},{8,10},{9,11},{10,... | collective-permute-start | bytes 122888 | tf_op jit(solution)/shard_map/ppermute | solution.py:186
  26.1 6.3 %collective-permute-start.9 = (bf16[40,512]{1,0:T(8,128)(2,1)S(1)}, bf16[40,512]{1,0:T(8,128)(2,1)S(1)}, u32[]{:S(2)}, u32[]{:S(2)}) collective-permute-start(bf16[40,512]{1,0:T(8,128)(2,1)S(1)} %get-tuple-element.16), channel_id=1, source_target_pairs={{0,3},{1,2},{2,1},{3,0},{4,7},{5,6},{6,5},{7,4},{8,11},{9,10},{10,... | collective-permute-start | bytes 122888 | tf_op jit(solution)/shard_map/ppermute | solution.py:186
  27.5 7.6 %collective-permute-start.6 = (bf16[104,512]{1,0:T(8,128)(2,1)S(1)}, bf16[104,512]{1,0:T(8,128)(2,1)S(1)}, u32[]{:S(2)}, u32[]{:S(2)}) collective-permute-start(bf16[104,512]{1,0:T(8,128)(2,1)S(1)} %get-tuple-element.13), channel_id=1, source_target_pairs={{0,1},{1,0},{2,3},{3,2},{4,5},{5,4},{6,7},{7,6},{8,9},{9,8},{10,11... | collective-permute-start | bytes 319496 | tf_op jit(solution)/shard_map/ppermute | solution.py:186
  27.8 7.3 %collective-permute-start.11 = (bf16[88,512]{1,0:T(8,128)(2,1)S(1)}, bf16[88,512]{1,0:T(8,128)(2,1)S(1)}, u32[]{:S(2)}, u32[]{:S(2)}) collective-permute-start(bf16[88,512]{1,0:T(8,128)(2,1)S(1)} %add_convert_fusion), channel_id=1, source_target_pairs={{0,2},{1,3},{2,0},{3,1},{4,6},{5,7},{6,4},{7,5},{8,10},{9,11},{10,... | collective-permute-start | bytes 270344 | tf_op jit(solution)/shard_map/ppermute | solution.py:186
